TPU v7x, 512 devices: a 8x2x16 block of a 8x8x16 slice. The times are simulated.
512 devices in a mesh: tile: 2 (over y), beam: 16 (over z), bl: 8 (over x), pol: 2 (over core).
Axes of the slice: x: 8, y: 2, z: 16, core: 2. Of those that a mesh axis runs over, the one named last changes fastest.
The devices are a block of a 8x8x16 slice.
Arguments:
- sky_model: bfloat16 [4096, 16384], P(('tile', 'bl', 'pol'), 'beam'), parts along dimension 0, may hold values from -6 to 6
- beam_pattern: bfloat16 [32, 2048, 2048], P(('tile', 'beam'), ('bl', 'pol')), parts along dimension 0, may hold values from 0.099609375 to 1
- kernels: bfloat16 [32, 1024, 128, 128], P(('tile', 'beam'), ('bl', 'pol')), parts along dimension 0, may hold values from -0.5 to 0.5
- observed: float32 [32, 1024, 2, 128], P(('tile', 'beam'), ('bl', 'pol')), parts along dimension 0, may hold values from -6 to 6
- tile_owner: int32 [32, 1024, 1], P(('tile', 'beam'), ('bl', 'pol')), parts along dimension 0, may hold values from 0 to 15; in each aligned block of 64 rows (0 to 63, 64 to 127, ..., all dimensions but the last counted through in order) at most 8 rows name the same one
- tile_local: int32 [32, 1024], P(('tile', 'beam'), ('bl', 'pol')), parts along dimension 0, may hold values from 0 to 1023
- vis_count: int32 [32, 1024], P(('tile', 'beam'), ('bl', 'pol')), parts along dimension 0, may hold values from 1 to 128
Outputs:
- residual_vis: float32 [32, 1024, 2, 128], P(('tile', 'beam'), ('bl', 'pol')), parts along dimension 0
- dirty_grid: float32 [32, 16384, 2, 128], P(('tile', 'beam'), ('bl', 'pol')), parts along dimension 0
There are 2 independent parts, one for each index of `tile`. A program takes and returns all parts, laid end to end along the dimension named above; each array names one. Nothing has to cross between parts.
Inputs may be any that keep to these rules, and one draw needn't show every extreme that they name: `tile_owner`: among the 64 visibility tiles of one device, at most 8 name the same owner, and in some blocks one owner is named exactly 8 times.
All inputs are finite; a program needn't handle non-finite values.
Results may differ from a plain program's by a relative error of at most 0.0055.
Values may be sent and summed in bfloat16 or wider, within the bound.
No kernel may reach another device: no remote copies, remote signals or barrier semaphores. Data moves between devices by JAX's collectives and lax.ppermute only.
A program may use at most 64 MiB of HBM per device.

v0:
```python
import math

import jax
import jax.numpy as jnp
from jax import lax
from jax.sharding import PartitionSpec as P

GRID = 2048
HALO = 512


def extended(block, sides, width):
    for axis, dim in sides:
        count = lax.axis_size(axis)
        forward = [(i, i + 1) for i in range(count - 1)]
        backward = [(target, source) for source, target in forward]
        low = lax.ppermute(
            lax.slice_in_dim(block, block.shape[dim] - width, None, axis=dim), axis, forward
        )
        high = lax.ppermute(lax.slice_in_dim(block, 0, width, axis=dim), axis, backward)
        block = jnp.concatenate([low, block, high], axis=dim)
    return block


def tables(rows, cols):
    row_index = jnp.arange(rows, dtype=jnp.int32)[:, None]
    col_index = jnp.arange(cols, dtype=jnp.int32)[None, :]
    angles = (row_index * col_index % GRID).astype(jnp.float32) * jnp.float32(2.0 * math.pi / GRID)
    factor = jnp.float32(1.0 / math.sqrt(GRID))
    return (
        (jnp.cos(angles) * factor).astype(jnp.bfloat16),
        (jnp.sin(angles) * factor).astype(jnp.bfloat16),
    )


def transform(table, image):
    return jnp.einsum("kux,yx->kuy", table, image, preferred_element_type=jnp.float32)


def weighted(pattern, values):
    return (pattern * values.astype(jnp.float32)).astype(jnp.bfloat16)


def on_device(sky_model, beam_pattern, kernels, observed, tile_owner, tile_local, vis_count):
    group = lax.axis_size(("bl", "pol"))
    cos_one, sin_one = tables(GRID // 2, GRID)
    first_table = jnp.stack([cos_one, -sin_one])
    pattern = beam_pattern[0].astype(jnp.float32)
    padded = extended(sky_model, (("beam", 1),), HALO)
    half_sum = transform(first_table, weighted(pattern, padded))
    half_plane = half_sum.astype(jnp.bfloat16)
    columns = lax.all_to_all(half_plane, ("bl", "pol"), split_axis=1, concat_axis=2, tiled=True)
    cos_two, sin_two = tables(GRID, GRID)
    real_part = columns[0]
    imag_part = columns[1]
    uv_real = jnp.dot(real_part, cos_two, preferred_element_type=jnp.float32) + jnp.dot(
        imag_part, sin_two, preferred_element_type=jnp.float32
    )
    uv_imag = jnp.dot(imag_part, cos_two, preferred_element_type=jnp.float32) - jnp.dot(
        real_part, sin_two, preferred_element_type=jnp.float32
    )
    uv_grid = jnp.stack([uv_real, uv_imag]).astype(jnp.bfloat16)
    u_rows = uv_grid.shape[1]
    cells = kernels.shape[3]
    grid_tiles = (
        uv_grid.reshape(2, u_rows // 8, 8, GRID // 16, 16)
        .transpose(1, 3, 0, 2, 4)
        .reshape(-1, 2, cells)
    )
    tiles_dev = grid_tiles.shape[0]
    owners = tile_owner[0, :, 0]
    local_ids = tile_local[0]
    vis_tiles = owners.shape[0]
    capacity = max(2, 2 * vis_tiles // group)
    onehot_owner = (owners[:, None] == jnp.arange(group, dtype=jnp.int32)[None, :]).astype(
        jnp.int32
    )
    ranking = jnp.cumsum(onehot_owner, axis=0) - onehot_owner
    slots = jnp.sum(ranking * onehot_owner, axis=1)
    destination = owners * capacity + slots
    request_ids = (
        jnp.full((group * capacity,), -1, jnp.int32)
        .at[destination]
        .set(local_ids)
        .reshape(group, capacity)
    )
    picked = grid_tiles[
        jnp.clip(
            lax.all_to_all(request_ids, ("bl", "pol"), split_axis=0, concat_axis=0, tiled=True),
            0,
            tiles_dev - 1,
        )
    ]
    returned = lax.all_to_all(picked, ("bl", "pol"), split_axis=0, concat_axis=0, tiled=True)
    fetched = returned.reshape(group * capacity, 2, cells)[destination]
    kernel_set = kernels[0]
    predicted = jnp.einsum("rjm,rcm->rcj", kernel_set, fetched, preferred_element_type=jnp.float32)
    live_mask = jnp.arange(cells, dtype=jnp.int32)[None, :] < vis_count[0][:, None]
    residual = jnp.where(live_mask[:, None, :], observed[0] - predicted, jnp.zeros_like(predicted))
    residual_low = residual.astype(jnp.bfloat16)
    contribution = jnp.einsum(
        "rjm,rcj->rcm", kernel_set, residual_low, preferred_element_type=jnp.float32
    )
    send_terms = (
        jnp.zeros((group * capacity, 2, cells), jnp.float32)
        .at[destination]
        .set(contribution)
        .reshape(group, capacity, 2, cells)
    )
    arrived, arrived_ids = (
        lax.all_to_all(
            send_terms.astype(jnp.bfloat16), ("bl", "pol"), split_axis=0, concat_axis=0, tiled=True
        ).astype(send_terms.dtype),
        lax.all_to_all(request_ids, ("bl", "pol"), split_axis=0, concat_axis=0, tiled=True),
    )
    flat_ids = arrived_ids.reshape(-1)
    valid = flat_ids >= 0
    terms = jnp.where(
        valid[:, None, None],
        arrived.reshape(-1, 2, cells),
        jnp.zeros((flat_ids.shape[0], 2, cells), jnp.float32),
    )
    dirty = (
        jnp.zeros((tiles_dev, 2, cells), jnp.float32)
        .at[jnp.clip(flat_ids, 0, tiles_dev - 1)]
        .add(terms)
    )
    return (residual[None], dirty[None])


def solution(mesh):
    placed = (
        P(("tile", "bl", "pol"), "beam"),
        P(("tile", "beam"), ("bl", "pol"), None),
        P(("tile", "beam"), ("bl", "pol"), None, None),
        P(("tile", "beam"), ("bl", "pol"), None, None),
        P(("tile", "beam"), ("bl", "pol"), None),
        P(("tile", "beam"), ("bl", "pol")),
        P(("tile", "beam"), ("bl", "pol")),
    )
    return jax.shard_map(
        on_device,
        mesh=mesh,
        in_specs=placed,
        out_specs=(
            P(("tile", "beam"), ("bl", "pol"), None, None),
            P(("tile", "beam"), ("bl", "pol"), None, None),
        ),
        check_vma=False,
    )
```

profile of v0, /device:TPU:65, one launch (start us, length us, event | category | flops | bytes accessed | tf_op | source)
XLA Modules:
  0.0 455.2 jit_solution(14030536862470296543)
XLA Ops:
  1.8 6.6 %collective-permute-start = (bf16[128,512]{1,0:T(8,128)(2,1)S(1)}, bf16[128,512]{1,0:T(8,128)(2,1)S(1)}, u32[]{:S(2)}, u32[]{:S(2)}) collective-permute-start(bf16[128,512]{1,0:T(8,128)(2,1)S(1)} %get-tuple-element.4), channel_id=1, source_target_pairs={{0,16},{16,32},{32,48},{48,64},{64,80},{80,96},{96,112},{112,128},... | collective-permute-start | bytes 393224 | tf_op jit(solution)/shard_map/ppermute | solution.py:17
  8.4 1.3 collective-permute-start.1
  13.6 39.4 %all-to-all-start.1 = ((s32[16,1,8]{2,1,0:T(1,128)}), s32[16,1,8]{2,1,0:T(1,128)S(1)}, u32[]{:S(2)}, u32[]{:S(2)}) async-start(s32[16,1,8]{2,1,0:T(1,128)} %bitcast.12), calls=%async_computation.1 | async-start | bytes 16384 | tf_op jit(solution)/shard_map/all_to_all | solution.py:89
  53.1 31.2 %fusion.20 = bf16[1,1024,2048]{2,1,0:T(8,128)(2,1)S(1)} fusion(), kind=kLoop, calls=%fused_computation.35 | loop fusion | flops 39845888 | bytes 4194304 | tf_op jit(solution)/shard_map/neg | solution.py:47
  84.3 31.0 %multiply_convert_fusion.7 = bf16[1,1024,2048]{2,1,0:T(8,128)(2,1)S(1)} fusion(), kind=kLoop, calls=%fused_computation.31 | loop fusion | flops 33554432 | bytes 4194304 | tf_op jit(solution)/shard_map/convert_element_type | solution.py:31
  115.4 2.4 fusion.29
  117.7 1.3 copy.22
  119.1 7.4 %all-to-all-start = ((bf16[2,1024,128]{2,0,1:T(2,128)(2,1)}), bf16[2,1024,128]{2,0,1:T(2,128)(2,1)S(1)}, u32[]{:S(2)}, u32[]{:S(2)}) async-start(bf16[2,1024,128]{2,0,1:T(2,128)(2,1)} %copy.22), calls=%async_computation | async-start | bytes 1048576 | tf_op jit(solution)/shard_map/all_to_all | solution.py:52
  127.0 16.7 %all-to-all-done = bf16[2,1024,128]{2,0,1:T(2,128)(2,1)S(1)} async-done(((bf16[2,1024,128]{2,0,1:T(2,128)(2,1)}), bf16[2,1024,128]{2,0,1:T(2,128)(2,1)S(1)}, u32[]{:S(2)}, u32[]{:S(2)}) %all-to-all-start) | async-done | bytes 524320 | tf_op jit(solution)/shard_map/all_to_all | solution.py:52
  144.0 62.5 %fusion.14 = f32[64,2048]{1,0:T(8,128)S(1)} fusion(bf16[8,8,16,128]{3,2,1,0:T(8,128)(2,1)S(1)} %bitcast.86), kind=kOutput, calls=%fused_computation.27 | convolution fusion | flops 603979776 | bytes 786432 | tf_op jit(solution)/shard_map/dot_general | solution.py:56
  206.5 74.3 %fusion.13 = f32[64,2048]{1,0:T(8,128)} fusion(bf16[8,8,16,128]{3,2,1,0:T(8,128)(2,1)S(1)} %bitcast.88), kind=kOutput, calls=%fused_computation.26 | convolution fusion | flops 603979776 | bytes 786432 | tf_op jit(solution)/shard_map/dot_general | solution.py:59
  280.8 63.3 %fusion.24 = bf16[64,2048]{1,0:T(8,128)(2,1)S(1)} fusion(f32[64,2048]{1,0:T(8,128)S(1)} %fusion.14, bf16[8,8,16,128]{3,2,1,0:T(8,128)(2,1)S(1)} %bitcast.89), kind=kOutput, calls=%fused_computation.39 | convolution fusion | flops 604241920 | bytes 1048576 | tf_op jit(solution)/shard_map/dot_general | solution.py:56
  344.2 2.7 stack.15
  346.9 1.9 copy.24
  348.8 64.4 %fusion.23 = bf16[64,2048]{1,0:T(8,128)(2,1)S(1)} fusion(f32[64,2048]{1,0:T(8,128)} %fusion.13, bf16[8,8,16,128]{3,2,1,0:T(8,128)(2,1)S(1)} %bitcast.87), kind=kOutput, calls=%fused_computation.38 | convolution fusion | flops 604241920 | bytes 1048576 | tf_op jit(solution)/shard_map/dot_general | solution.py:59
  413.2 2.7 stack.16
  416.0 1.9 copy.25
  420.3 3.9 all-to-all-start.2
  424.4 6.8 %all-to-all-done.2 = bf16[16,8,2,128]{3,1,2,0:T(8,128)(2,1)S(1)} async-done(((bf16[16,8,2,128]{3,1,2,0:T(8,128)(2,1)}), bf16[16,8,2,128]{3,1,2,0:T(8,128)(2,1)S(1)}, u32[]{:S(2)}, u32[]{:S(2)}) %all-to-all-start.2) | async-done | bytes 65568 | tf_op jit(solution)/shard_map/all_to_all | solution.py:94
  432.0 1.2 fusion.35
  433.9 2.4 scatter_fusion
  437.0 3.7 all-to-all-start.3
  440.7 7.8 %all-to-all-done.3 = bf16[16,8,2,128]{3,2,1,0:T(2,128)(2,1)S(1)} async-done(((bf16[16,8,2,128]{3,2,1,0:T(2,128)(2,1)}), bf16[16,8,2,128]{3,2,1,0:T(2,128)(2,1)S(1)}, u32[]{:S(2)}, u32[]{:S(2)}) %all-to-all-start.3) | async-done | bytes 65568 | tf_op jit(solution)/shard_map/all_to_all | solution.py:111
  448.9 5.1 %scatter_fusion.1 = f32[1024,2,128]{2,1,0:T(2,128)S(1)} fusion(f32[1024,2,128]{2,1,0:T(2,128)S(1)} %broadcast_in_dim.48, s32[128]{0:T(128)S(1)} %fusion.58, f32[128,2,128]{2,1,0:T(2,128)S(1)} %convert_select_fusion), kind=kCustom, calls=%fused_computation.4 | custom fusion | flops 32768 | bytes 393728 | tf_op jit(solution)/shard_map/scatter-add | solution.py:126
  (54 shorter events, 12.1 us)
Async XLA Ops:
  0.6 431.3 %copy-start = (bf16[1,64,128,128]{3,2,1,0:T(8,128)(2,1)S(1)}, bf16[1,64,128,128]{3,2,1,0:T(8,128)(2,1)}, u32[]{:S(2)}) copy-start(bf16[1,64,128,128]{3,2,1,0:T(8,128)(2,1)} %param.9) | copy-start | bytes 6291460
  1.8 113.5 %collective-permute-start = (bf16[128,512]{1,0:T(8,128)(2,1)S(1)}, bf16[128,512]{1,0:T(8,128)(2,1)S(1)}, u32[]{:S(2)}, u32[]{:S(2)}) collective-permute-start(bf16[128,512]{1,0:T(8,128)(2,1)S(1)} %get-tuple-element.4), channel_id=1, source_target_pairs={{0,16},{16,32},{32,48},{48,64},{64,80},{80,96},{96,112},{112,128},... | collective-permute-start | bytes 393224 | tf_op jit(solution)/shard_map/ppermute | solution.py:17
  8.4 107.0 %collective-permute-start.1 = (bf16[128,512]{1,0:T(8,128)(2,1)S(1)}, bf16[128,512]{1,0:T(8,128)(2,1)S(1)}, u32[]{:S(2)}, u32[]{:S(2)}) collective-permute-start(bf16[128,512]{1,0:T(8,128)(2,1)S(1)} %get-tuple-element.5), channel_id=1, source_target_pairs={{16,0},{32,16},{48,32},{64,48},{80,64},{96,80},{112,96},{128,112},... | collective-permute-start | bytes 393224 | tf_op jit(solution)/shard_map/ppermute | solution.py:20
  13.6 105.5 %all-to-all-start.1 = ((s32[16,1,8]{2,1,0:T(1,128)}), s32[16,1,8]{2,1,0:T(1,128)S(1)}, u32[]{:S(2)}, u32[]{:S(2)}) async-start(s32[16,1,8]{2,1,0:T(1,128)} %bitcast.12), calls=%async_computation.1 | async-start | bytes 16384 | tf_op jit(solution)/shard_map/all_to_all | solution.py:89
  53.1 62.3 %copy-start.3 = (bf16[128,1024]{1,0:T(8,128)(2,1)S(1)}, bf16[128,1024]{1,0:T(8,128)(2,1)}, u32[]{:S(2)}) copy-start(bf16[128,1024]{1,0:T(8,128)(2,1)} %param.7) | copy-start | bytes 786436
  53.1 62.3 %copy-start.6 = (bf16[1,128,2048]{2,1,0:T(8,128)(2,1)S(1)}, bf16[1,128,2048]{2,1,0:T(8,128)(2,1)}, u32[]{:S(2)}) copy-start(bf16[1,128,2048]{2,1,0:T(8,128)(2,1)} %param.8) | copy-start | bytes 1572868
  115.3 11.2 %copy-start.5 = (s32[1,64]{1,0:T(1,128)S(1)}, s32[1,64]{1,0:T(1,128)}, u32[]{:S(2)}) copy-start(s32[1,64]{1,0:T(1,128)} %param.13) | copy-start | bytes 772
  119.1 24.6 %all-to-all-start = ((bf16[2,1024,128]{2,0,1:T(2,128)(2,1)}), bf16[2,1024,128]{2,0,1:T(2,128)(2,1)S(1)}, u32[]{:S(2)}, u32[]{:S(2)}) async-start(bf16[2,1024,128]{2,0,1:T(2,128)(2,1)} %copy.22), calls=%async_computation | async-start | bytes 1048576 | tf_op jit(solution)/shard_map/all_to_all | solution.py:52
  416.0 16.0 %copy-start.4 = (f32[1,64,2,128]{3,2,1,0:T(2,128)S(1)}, f32[1,64,2,128]{3,2,1,0:T(2,128)}, u32[]{:S(2)}) copy-start(f32[1,64,2,128]{3,2,1,0:T(2,128)} %param.10) | copy-start | bytes 196612
  420.3 10.9 %all-to-all-start.2 = ((bf16[16,8,2,128]{3,1,2,0:T(8,128)(2,1)}), bf16[16,8,2,128]{3,1,2,0:T(8,128)(2,1)S(1)}, u32[]{:S(2)}, u32[]{:S(2)}) async-start(bf16[16,8,2,128]{3,1,2,0:T(8,128)(2,1)} %copy.32), calls=%async_computation.2 | async-start | bytes 131072 | tf_op jit(solution)/shard_map/all_to_all | solution.py:94
  433.1 20.9 %copy-start.2 = (f32[64,2,128]{2,1,0:T(2,128)}, f32[64,2,128]{2,1,0:T(2,128)S(1)}, u32[]{:S(2)}) copy-start(f32[64,2,128]{2,1,0:T(2,128)S(1)} %fusion.35) | copy-start | bytes 196612
  437.0 11.5 %all-to-all-start.3 = ((bf16[16,8,2,128]{3,2,1,0:T(2,128)(2,1)}), bf16[16,8,2,128]{3,2,1,0:T(2,128)(2,1)S(1)}, u32[]{:S(2)}, u32[]{:S(2)}) async-start(bf16[16,8,2,128]{3,2,1,0:T(2,128)(2,1)} %bitcast.19), calls=%async_computation.3 | async-start | bytes 131072 | tf_op jit(solution)/shard_map/all_to_all | solution.py:111
  454.0 1.0 copy-start.1
where the time goes:
time: 463 us; the launch traced here: 455 us
  matrix products  269 us (58%)
  other arithmetic  70.7 us (15%)
  starting transfers between devices  62.2 us (13%)
  waiting for transfers between devices  31.3 us (7%)
  local copies, waits for them, and re-layouts  21.1 us (5%)
    dot_general x1, matrix products, on_device(): jnp.dot(imag_part, cos_two, preferred_element_type=jnp.float32)  74.3 us
    dot_general x1, matrix products, on_device(): jnp.dot(real_part, sin_two, preferred_element_type=jnp.float32)  64.4 us
    dot_general x1, matrix products, on_device(): jnp.dot(imag_part, sin_two, preferred_element_type=jnp.float32)  63.3 us
    dot_general x1, matrix products, on_device(): jnp.dot(real_part, cos_two, preferred_element_type=jnp.float32)  62.5 us
    all_to_all x1, starting transfers between devices, on_device(): lax.all_to_all(request_ids, ('bl', 'pol'), split_axis=0, concat_axis=0, t...  39.4 us
    neg x1, other arithmetic, on_device(): first_table = jnp.stack([cos_one, -sin_one])  31.2 us
    convert_element_type x1, other arithmetic, tables(): (jnp.cos(angles) * factor).astype(jnp.bfloat16)  31 us
    all_to_all x1, waiting for transfers between devices, on_device(): lax.all_to_all(half_plane, ('bl', 'pol'), split_axis=1, concat_axis=2, ti...  16.7 us
  transfers between devices with their start and end apart: 6, of which 3 were waited for; matrix products, arithmetic and copies ran while one was open for 15% of the time, Pallas kernels for 0%

commit v1 on v0

v1 whole, which is shorter than its diff:
```python
import math

import jax
import jax.numpy as jnp
import numpy as np
from jax import lax
from jax.experimental import pallas as pl
from jax.experimental.pallas import tpu as pltpu
from jax.sharding import PartitionSpec as P

GRID = 2048
HALO = 512
RADIX = 16
LANES = GRID // RADIX
GROUP_AXES = ("bl", "pol")
F32 = jnp.float32
BF16 = jnp.bfloat16


def spin(re, im, k, n):
    k = k % n
    c, s = math.cos(2 * math.pi * k / n), math.sin(2 * math.pi * k / n)
    if k == 0:
        return re, im
    if 4 * k == n:
        return im, -re
    if im is None:
        return re * np.float32(c), re * np.float32(-s)
    if 8 * k == n:
        h = np.float32(math.sqrt(0.5))
        return (re + im) * h, (im - re) * h
    if 8 * k == 3 * n:
        h = np.float32(math.sqrt(0.5))
        return (im - re) * h, (re + im) * -h
    return re * np.float32(c) + im * np.float32(s), im * np.float32(c) - re * np.float32(s)


def plus(a, b):
    return b if a is None else a if b is None else a + b


def minus(a, b):
    return a if b is None else -b if a is None else a - b


def real_dft(x):
    n = len(x)
    if n == 1:
        return [(x[0], None)]
    if n == 2:
        return [(x[0] + x[1], None), (x[0] - x[1], None)]
    even, odd = real_dft(x[0::2]), real_dft(x[1::2])
    out = [None] * (n // 2 + 1)
    for k in range(n // 4 + 1):
        (er, ei), (orr, oi) = even[k], odd[k]
        if 4 * k == n:
            tr, ti = None, (None if orr is None else -orr)
        else:
            tr, ti = spin(orr, oi, k, n)
        out[k] = (plus(er, tr), plus(ei, ti))
        if n // 2 - k != k:
            low = minus(ei, ti)
            out[n // 2 - k] = (minus(er, tr), None if low is None else minus(None, low))
    return out


def complex_dft(x):
    n = len(x)
    if n == 1:
        return x
    even, odd = complex_dft(x[0::2]), complex_dft(x[1::2])
    low, high = [], []
    for k in range(n // 2):
        (er, ei), (tr, ti) = even[k], spin(odd[k][0], odd[k][1], k, n)
        low.append((er + tr, ei + ti))
        high.append((er - tr, ei - ti))
    return low + high


def first_table(group):
    half = RADIX // 2
    per = GRID // 2 // RADIX // group
    p, d, s, q = np.meshgrid(
        np.arange(half), np.arange(group), np.arange(2), np.arange(per), indexing="ij"
    )
    u1 = np.where(s == 0, p, np.where(p == 0, half, RADIX - p))
    u = RADIX * (per * d + q) + u1
    x0 = np.arange(LANES)
    angle = 2 * np.pi * ((u[..., None] * x0) % GRID) / GRID
    c, n = np.cos(angle) / math.sqrt(GRID), np.sin(angle) / math.sqrt(GRID)
    first = (p == 0)[..., None]
    side = (s == 0)[..., None]
    sign = np.where(side, 1.0, -1.0)
    rr = np.where(first, np.where(side, c, 0.0), c)
    ri = np.where(first, np.where(side, 0.0, c), sign * n)
    ir = np.where(first, np.where(side, -n, 0.0), -n)
    ii = np.where(first, np.where(side, 0.0, -n), sign * c)
    real = np.concatenate([rr, ri], axis=-1)
    imag = np.concatenate([ir, ii], axis=-1)
    both = np.stack([real, imag], axis=2)
    return both.reshape(half, group * 2 * 2 * per, 2 * LANES).astype(np.float32).astype(BF16)


def second_table():
    v1, y0, v0 = np.meshgrid(np.arange(RADIX), np.arange(LANES), np.arange(LANES), indexing="ij")
    angle = 2 * np.pi * ((y0 * (RADIX * v0 + v1)) % GRID) / GRID
    c, n = np.cos(angle) / math.sqrt(GRID), np.sin(angle) / math.sqrt(GRID)
    top = np.concatenate([c, -n], axis=2)
    low = np.concatenate([n, c], axis=2)
    return np.concatenate([top, low], axis=1).astype(np.float32).astype(BF16)


def placing(rows):
    row = np.arange(rows)
    p, s = row // 8, (row // 4) % 2
    i = np.where(s == 0, p, (8 - p) % 8)
    out = np.zeros((8 * RADIX, RADIX, rows), np.float32)
    for v1 in range(RADIX):
        out[RADIX * i + v1, v1, row] = 1.0
    return out.reshape(8 * RADIX, RADIX * rows).astype(BF16)


def dot(a, b, dims=((1,), (0,))):
    return lax.dot_general(a, b, (dims, ((), ())), preferred_element_type=F32)


def iota(shape, dim):
    return lax.broadcasted_iota(jnp.int32, shape, dim)


def plan_body(
    owner_ref, local_ref, count_ref, sky_any, pattern_any, table_any,
    ids_ref, pick_ref, put_ref, live_ref, sky_ref, pattern_ref, table_ref, sems,
):
    copies = [
        pltpu.make_async_copy(source, target, sems.at[i])
        for i, (source, target) in enumerate(
            [(sky_any, sky_ref), (pattern_any, pattern_ref), (table_any, table_ref)]
        )
    ]
    for copy in copies:
        copy.start()
    n = owner_ref.shape[0]
    group, cap = ids_ref.shape
    owner_col = owner_ref[...].astype(F32)
    local_row = local_ref[...].astype(F32)
    count_row = count_ref[...].astype(F32)
    eye = iota((n, n), 0) == iota((n, n), 1)
    owner_row = jnp.sum(jnp.where(eye, owner_col, 0.0), axis=0, keepdims=True)
    same = owner_col == owner_row
    before = jnp.where(same & (iota((n, n), 0) < iota((n, n), 1)), 1.0, 0.0)
    slot_row = jnp.sum(before, axis=0, keepdims=True)
    after = jnp.where(same & (iota((n, n), 1) < iota((n, n), 0)), 1.0, 0.0)
    slot_col = jnp.sum(after, axis=1, keepdims=True)
    mine = iota((group, n), 0).astype(F32) == owner_row
    ids = jnp.zeros((group, cap), F32)
    for k in range(cap):
        hit = jnp.where(mine & (slot_row == float(k)), local_row + 1.0, 0.0)
        ids = jnp.where(iota((group, cap), 1) == k, jnp.sum(hit, axis=1, keepdims=True), ids)
    ids_ref[...] = ids.astype(jnp.int32) - 1
    target_row = owner_row * float(2 * cap) + slot_row
    target_col = owner_col * float(2 * cap) + slot_col
    rows, wide = pick_ref.shape
    mid = jnp.where(iota((rows, n), 0) // 2 == iota((rows, n), 1), 1.0, 0.0)
    col = jnp.sum(mid * target_row, axis=1, keepdims=True)
    col = col + (iota((rows, 1), 0) % 2 * cap).astype(F32)
    pick_ref[...] = jnp.where(iota((rows, wide), 1).astype(F32) == col, 1.0, 0.0).astype(BF16)
    dim = jnp.where(iota((n, rows), 1) // 2 == iota((n, rows), 0), 1.0, 0.0)
    row = jnp.sum(dim * target_col, axis=0, keepdims=True)
    row = row + (iota((1, rows), 1) % 2 * cap).astype(F32)
    put_ref[...] = jnp.where(iota((wide, rows), 0).astype(F32) == row, 1.0, 0.0).astype(BF16)
    count = jnp.sum(mid * count_row, axis=1, keepdims=True)
    live_ref[...] = jnp.where(iota(live_ref.shape, 1).astype(F32) < count, 1.0, 0.0)
    for copy in copies:
        copy.wait()


def first_body(low_ref, sky_ref, high_ref, pattern_ref, table_ref, out_any, mid_ref, out_ref, sems):
    rows = sky_ref.shape[0]
    block = 16
    for start in range(0, rows, block):
        at = slice(start, start + block)
        parts = []
        for x1 in range(RADIX):
            lo = x1 * LANES
            if lo < HALO:
                sky = low_ref[at, lo : lo + LANES]
            elif lo < GRID - HALO:
                sky = sky_ref[at, lo - HALO : lo - HALO + LANES]
            else:
                sky = high_ref[at, lo - GRID + HALO : lo - GRID + HALO + LANES]
            seen = pattern_ref[at, lo : lo + LANES].astype(F32) * sky.astype(F32)
            parts.append(seen.astype(BF16).astype(F32))
        out = real_dft(parts)
        mid_ref[0, at, :LANES] = out[0][0].astype(BF16)
        mid_ref[0, at, LANES:] = out[RADIX // 2][0].astype(BF16)
        for p in range(1, RADIX // 2):
            mid_ref[p, at, :LANES] = out[p][0].astype(BF16)
            mid_ref[p, at, LANES:] = out[p][1].astype(BF16)
    group = out_ref.shape[1]
    copies = []
    for p in range(RADIX // 2):
        half = dot(table_ref[p], mid_ref[p], ((1,), (1,)))
        per = half.shape[0] // group
        out_ref[p] = half.reshape(group, per, rows).astype(BF16)
        copies.append(
            pltpu.make_async_copy(
                out_ref.at[p], out_any.at[:, p * per : (p + 1) * per, :], sems.at[p]
            )
        )
        copies[-1].start()
    for copy in copies:
        copy.wait()


def second_body(half_ref, ids_ref, table_any, place_any, out_ref, table_ref, place_ref, mid_ref, sel_ref, sems):
    copies = [
        pltpu.make_async_copy(table_any.at[v1], table_ref.at[v1], sems.at[v1])
        for v1 in range(RADIX)
    ]
    copies.append(pltpu.make_async_copy(place_any, place_ref, sems.at[RADIX]))
    for copy in copies:
        copy.start()
    group = half_ref.shape[0]
    rows = mid_ref.shape[1]
    for pair in range(rows // 16):
        done = []
        for p in (2 * pair, 2 * pair + 1):
            parts = []
            for y1 in range(group):
                both = half_ref[y1, 16 * p : 16 * p + 16, :].astype(F32)
                parts.append((both[:8], both[8:]))
            done.append(complex_dft(parts))
        at = slice(16 * pair, 16 * pair + 16)
        for v1 in range(RADIX):
            for c in range(2):
                both = jnp.concatenate([done[0][v1][c], done[1][v1][c]], axis=0)
                mid_ref[v1, at, c * LANES : (c + 1) * LANES] = both.astype(BF16)
    ids = ids_ref[...]
    wanted = ids.shape[1]
    hot = jnp.where(iota((LANES, wanted), 0) == ids % LANES, 1.0, 0.0).astype(BF16)
    row = iota((rows, wanted), 0)
    mask = jnp.where(2 * (row % 4) + row // 4 % 2 == ids // LANES, 1.0, 0.0)
    for v1 in range(RADIX):
        copies[v1].wait()
        grid = dot(mid_ref[v1], table_ref[v1]).astype(BF16)
        for c in range(2):
            got = dot(grid[:, c * LANES : (c + 1) * LANES], hot)
            sel_ref[c, v1 * rows : (v1 + 1) * rows, :] = (got * mask).astype(BF16)
    copies[RADIX].wait()
    tiles = []
    for c in range(2):
        got = dot(place_ref[...], sel_ref[c])
        tiles.append(got.T.reshape(group, wanted // group, got.shape[0]))
    out_ref[...] = jnp.concatenate(tiles, axis=1).astype(BF16)


def visit_body(
    tiles_ref, pick_ref, put_ref, live_ref, seen_ref, kernel_any, res_ref, out_ref, kernel_ref, sems
):
    cells = kernel_ref.shape[1]
    rows = seen_ref.shape[0]
    size = 4 * cells
    copies = [
        pltpu.make_async_copy(
            kernel_any.at[pl.ds(g * size, size)], kernel_ref.at[pl.ds(g * size, size)], sems.at[g]
        )
        for g in range(rows // 8)
    ]
    for copy in copies:
        copy.start()
    fetched = dot(pick_ref[...], tiles_ref[...])
    of = iota((8, cells), 0) // 2
    terms = []
    for g in range(rows // 8):
        at = slice(8 * g, 8 * g + 8)
        own = fetched[at]
        guess = jnp.zeros((8, cells), F32)
        copies[g].wait()
        for h in range(2):
            left = jnp.concatenate(
                [jnp.where(of == 2 * h + q, own, 0.0) for q in range(2)], axis=1
            ).astype(BF16)
            first = (4 * g + 2 * h) * cells
            right = jnp.concatenate(
                [kernel_ref[first : first + cells], kernel_ref[first + cells : first + 2 * cells]],
                axis=1,
            )
            guess = guess + dot(left, right, ((1,), (1,)))
        res = jnp.where(live_ref[at] > 0.0, seen_ref[at] - guess, 0.0)
        res_ref[at] = res
        term = jnp.zeros((8, cells), F32)
        for h in range(2):
            left = jnp.concatenate(
                [jnp.where(of == 2 * h + q, res, 0.0) for q in range(2)], axis=1
            ).astype(BF16)
            first = (4 * g + 2 * h) * cells
            term = term + dot(left, kernel_ref[first : first + 2 * cells])
        terms.append(term)
    term = jnp.concatenate(terms, axis=0).astype(BF16)
    out_ref[...] = dot(put_ref[...], term).astype(BF16)


def dirty_body(term_ref, target_ref, out_any, out_ref, sems):
    rows = out_ref.shape[0]
    step = rows // sems.shape[0]
    target = target_ref[...]
    term = term_ref[...]
    copies = []
    for i in range(sems.shape[0]):
        at = pl.ds(i * step, step)
        hot = jnp.where(iota((step, target.shape[1]), 0) + i * step == target, 1.0, 0.0)
        out_ref[at, :] = dot(hot.astype(BF16), term)
        copies.append(pltpu.make_async_copy(out_ref.at[at], out_any.at[at], sems.at[i]))
        copies[-1].start()
    for copy in copies:
        copy.wait()


FAST = pltpu.VMEM
ANY = pl.ANY


def call(body, name, outs, args, scratch=()):
    shapes = [
        pltpu.VMEM(s, d) if space is FAST else jax.ShapeDtypeStruct(s, d) for s, d, space in outs
    ]
    spec = lambda space: pl.BlockSpec(memory_space=pltpu.VMEM if space is None else space)
    return pl.pallas_call(
        body,
        out_shape=shapes,
        in_specs=[spec(space) for _, space in args],
        out_specs=[spec(space) for _, _, space in outs],
        scratch_shapes=list(scratch),
        name=name,
    )(*[pltpu.with_memory_space_constraint(a, FAST) if space is FAST else a for a, space in args])


def exchange(block):
    return lax.all_to_all(block, GROUP_AXES, split_axis=0, concat_axis=0, tiled=True)


def on_device(sky_model, beam_pattern, kernels, observed, tile_owner, tile_local, vis_count):
    group = lax.axis_size(GROUP_AXES)
    rows, strip = sky_model.shape
    vis, cells = kernels.shape[1], kernels.shape[3]
    cap = max(2, 2 * vis // group)
    u_rows = GRID // 2 // group
    tiles_dev = u_rows // 8 * (GRID // 16)
    sem = pltpu.SemaphoreType.DMA

    count = lax.axis_size("beam")
    forward = [(i, i + 1) for i in range(count - 1)]
    backward = [(target, source) for source, target in forward]
    low = lax.ppermute(sky_model[:, strip - HALO :], "beam", forward)
    high = lax.ppermute(sky_model[:, :HALO], "beam", backward)

    table = first_table(group)
    ids, pick, put, live, sky_fast, pattern_fast, table_fast = call(
        plan_body,
        "plan",
        [
            ((group, cap), jnp.int32, None),
            ((2 * vis, 2 * group * cap), BF16, FAST),
            ((2 * group * cap, 2 * vis), BF16, FAST),
            ((2 * vis, cells), F32, FAST),
            ((rows, strip), BF16, FAST),
            ((rows, GRID), BF16, FAST),
            (table.shape, BF16, FAST),
        ],
        [
            (tile_owner[0], None),
            (tile_local, None),
            (vis_count, None),
            (sky_model, ANY),
            (beam_pattern[0], ANY),
            (table, ANY),
        ],
        [sem((3,))],
    )
    asked = exchange(ids)
    asked_row = asked.reshape(1, group * cap)
    target = jnp.concatenate([2 * asked, 2 * asked + 1], axis=1).reshape(1, 2 * group * cap)

    (half,) = call(
        first_body,
        "first",
        [((group, 2 * u_rows, rows), BF16, ANY)],
        [(low, FAST), (sky_fast, FAST), (high, FAST), (pattern_fast, FAST), (table_fast, FAST)],
        [
            pltpu.VMEM((RADIX // 2, rows, 2 * LANES), BF16),
            pltpu.VMEM((RADIX // 2, group, 2 * u_rows // 8, rows), BF16),
            sem((RADIX // 2,)),
        ],
    )
    columns = exchange(half)
    table = second_table()
    place = placing(u_rows)
    (tiles,) = call(
        second_body,
        "second",
        [((group, 2 * cap, cells), BF16, None)],
        [(columns, FAST), (asked_row, FAST), (table, ANY), (place, ANY)],
        [
            pltpu.VMEM(table.shape, BF16),
            pltpu.VMEM(place.shape, BF16),
            pltpu.VMEM((RADIX, u_rows, 2 * LANES), BF16),
            pltpu.VMEM((2, RADIX * u_rows, group * cap), BF16),
            sem((RADIX + 1,)),
        ],
    )
    returned = exchange(tiles)
    residual, terms = call(
        visit_body,
        "visit",
        [((2 * vis, cells), F32, None), ((2 * group * cap, cells), BF16, None)],
        [
            (returned.reshape(2 * group * cap, cells), FAST),
            (pick, FAST),
            (put, FAST),
            (live, FAST),
            (observed.reshape(2 * vis, cells), FAST),
            (kernels.reshape(vis * cells, cells), ANY),
        ],
        [pltpu.VMEM((vis * cells, cells), BF16), sem((vis // 4,))],
    )
    arrived = exchange(terms.reshape(group, 2 * cap, cells))
    (dirty,) = call(
        dirty_body,
        "dirty",
        [((2 * tiles_dev, cells), F32, ANY)],
        [(arrived.reshape(2 * group * cap, cells), FAST), (target, FAST)],
        [pltpu.VMEM((2 * tiles_dev, cells), F32), sem((8,))],
    )
    return residual.reshape(1, vis, 2, cells), dirty.reshape(1, tiles_dev, 2, cells)


def solution(mesh):
    placed = (
        P(("tile", "bl", "pol"), "beam"),
        P(("tile", "beam"), ("bl", "pol"), None),
        P(("tile", "beam"), ("bl", "pol"), None, None),
        P(("tile", "beam"), ("bl", "pol"), None, None),
        P(("tile", "beam"), ("bl", "pol"), None),
        P(("tile", "beam"), ("bl", "pol")),
        P(("tile", "beam"), ("bl", "pol")),
    )
    return jax.shard_map(
        on_device,
        mesh=mesh,
        in_specs=placed,
        out_specs=(
            P(("tile", "beam"), ("bl", "pol"), None, None),
            P(("tile", "beam"), ("bl", "pol"), None, None),
        ),
        check_vma=False,
    )
```

time: 463 us -> 119 us (0.26); the launches traced: 455 us -> 119 us
  matrix products: 269 us -> 0 us
  other arithmetic: 70.7 us -> 0.68 us
  Pallas kernels: 0 us -> 19.2 us
  local copies, waits for them, and re-layouts: 21.1 us -> 3.17 us
  waiting for transfers between devices: 31.3 us -> 36.3 us
    dot_general x7 -> x0, matrix products: 269 us -> none  [the longest x1 74.3 us: on_device(): jnp.dot(imag_part, cos_two, preferred_element_type=jnp.float32)]
    convert_element_type x3 -> x0, other arithmetic: 32.4 us -> none  [the longest x1 31 us: tables(): (jnp.cos(angles) * factor).astype(jnp.bfloat16)]
    neg x1 -> x0, other arithmetic: 31.2 us -> none  [on_device(): first_table = jnp.stack([cos_one, -sin_one])]
    pallas_call x0 -> x5, Pallas kernels: none -> 19.2 us  [call(): pl.pallas_call(body, out_shape=shapes, in_specs=[spec(space) for _, space...]
    another operation x5 -> x0, local copies, waits for them, and re-layouts: 9.29 us -> none  [the longest x4 9.25 us: on_device(): uv_grid = jnp.stack([uv_real, uv_imag]).astype(jnp.bfloat16)]
    scatter-add x1 -> x0, other arithmetic: 5.09 us -> none  [on_device(): dirty = jnp.zeros((tiles_dev, 2, cells), jnp.float32).at[jnp.clip(flat_id...]
    all_to_all x4, waiting for transfers between devices: 31.3 us -> 36.3 us  [exchange(): lax.all_to_all(block, GROUP_AXES, split_axis=0, concat_axis=0, tiled=True)]
  transfers between devices with their start and end apart: 6 -> 6, of which waited for: 3 -> 4; matrix products, arithmetic and copies ran while one was open for 15% -> 2% of each run, Pallas kernels for 0% -> 4%
where the time goes in v1:
time: 119 us
  starting transfers between devices  58.7 us (49%)
  waiting for transfers between devices  36.3 us (31%)
  Pallas kernels  19.2 us (16%)
  local copies, waits for them, and re-layouts  3.17 us (3%)
    all_to_all x4, starting transfers between devices, exchange(): lax.all_to_all(block, GROUP_AXES, split_axis=0, concat_axis=0, tiled=True)  50.9 us
    all_to_all x4, waiting for transfers between devices, exchange(): lax.all_to_all(block, GROUP_AXES, split_axis=0, concat_axis=0, tiled=True)  36.3 us
    pallas_call x5, Pallas kernels, call(): pl.pallas_call(body, out_shape=shapes, in_specs=[spec(space) for _, space...  19.2 us
    ppermute x1, starting transfers between devices, on_device(): low = lax.ppermute(sky_model[:, strip - HALO:], 'beam', forward)  6.57 us
  transfers between devices with their start and end apart: 6, of which 4 were waited for; matrix products, arithmetic and copies ran while one was open for 2% of the time, Pallas kernels for 4%

profile of v1, /device:TPU:65, one launch (start us, length us, event | category | flops | bytes accessed | tf_op | source)
XLA Modules:
  0.0 118.9 jit_solution(11307754395436103041)
XLA Ops:
  0.6 1.0 fusion
  1.6 6.6 %collective-permute-start = (bf16[128,512]{1,0:T(8,128)(2,1)S(1)}, bf16[128,512]{1,0:T(8,128)(2,1)S(1)}, u32[]{:S(2)}, u32[]{:S(2)}) collective-permute-start(bf16[128,512]{1,0:T(8,128)(2,1)S(1)} %get-tuple-element.21), channel_id=1, source_target_pairs={{0,16},{16,32},{32,48},{48,64},{64,80},{80,96},{96,112},{112,128},... | collective-permute-start | bytes 393224 | tf_op jit(solution)/shard_map/ppermute | solution.py:355
  8.2 1.3 %collective-permute-start.1 = (bf16[128,512]{1,0:T(8,128)(2,1)S(1)}, bf16[128,512]{1,0:T(8,128)(2,1)S(1)}, u32[]{:S(2)}, u32[]{:S(2)}) collective-permute-start(bf16[128,512]{1,0:T(8,128)(2,1)S(1)} %get-tuple-element.20), channel_id=1, source_target_pairs={{16,0},{32,16},{48,32},{64,48},{80,64},{96,80},{112,96},{128,112},... | collective-permute-start | bytes 393224 | tf_op jit(solution)/shard_map/ppermute | solution.py:356
  9.5 1.4 %copy.20.owner_ref = s32[64,1]{1,0:T(8,128)} copy(s32[64,1]{0,1:T(1,128)} %bitcast.24) | data formatting | bytes 512 | tf_op jit(solution)/shard_map/squeeze | solution.py:372
  10.9 2.9 %plan.1 = (s32[16,8]{1,0:T(8,128)}, bf16[128,256]{1,0:T(8,128)(2,1)S(1)}, bf16[256,128]{1,0:T(8,128)(2,1)S(1)}, f32[128,128]{1,0:T(8,128)S(1)}, bf16[128,1024]{1...) custom-call(s32[64,1]{1,0:T(8,128)} %copy.20.owner_ref, s32[1,64]{1,0:T(1,128)} %local_ref.1, ...), custom_call_target="tpu_custom_call" | custom-call | tf_op jit(solution)/shard_map/plan/pallas_call | solution.py:329
  13.7 39.5 %all-to-all-start.1 = ((s32[16,1,8]{2,1,0:T(1,128)}), s32[16,1,8]{2,1,0:T(1,128)S(1)}, u32[]{:S(2)}, u32[]{:S(2)}) async-start(s32[16,1,8]{2,1,0:T(1,128)} %bitcast.23), calls=%async_computation.1 | async-start | bytes 16384 | tf_op jit(solution)/shard_map/all_to_all | solution.py:340
  53.2 1.4 %first.1 = bf16[16,128,128]{2,1,0:T(8,128)(2,1)} custom-call(bf16[128,512]{1,0:T(8,128)(2,1)S(1)} %collective-permute-done.low_ref, bf16[128,1024]{1,0:T(8,128)(2,1)S(1)} %get-tuple-element.11.sky_ref, bf16[128,512]{1,0:T(8,128)(2,1)S(1)} %collective-permute-done.1.high_ref, bf16[128,2048]{1,0:T(8,128)(2,1)S(1)} %get-tuple-element.12.pattern_ref, ...), custom_call_target="tpu_custom_call" | custom-call | tf_op jit(solution)/shard_map/first/pallas_call | solution.py:329
  54.7 0.0 copy-start
  54.7 5.7 %all-to-all-done.1 = s32[16,1,8]{2,1,0:T(1,128)S(1)} async-done(((s32[16,1,8]{2,1,0:T(1,128)}), s32[16,1,8]{2,1,0:T(1,128)S(1)}, u32[]{:S(2)}, u32[]{:S(2)}) %all-to-all-start.1) | async-done | bytes 544 | tf_op jit(solution)/shard_map/all_to_all | solution.py:340
  60.4 4.0 %all-to-all-start = ((bf16[16,128,128]{2,1,0:T(8,128)(2,1)}), bf16[16,128,128]{2,1,0:T(8,128)(2,1)S(1)}, u32[]{:S(2)}, u32[]{:S(2)}) async-start(bf16[16,128,128]{2,1,0:T(8,128)(2,1)} %first.1), calls=%async_computation | async-start | bytes 1048576 | tf_op jit(solution)/shard_map/all_to_all | solution.py:340
  64.4 0.5 broadcast.12
  64.9 0.7 reduce.3
  65.6 0.1 reshape.36.ids_ref
  65.7 0.1 copy.23
  65.8 15.9 %all-to-all-done.half_ref = bf16[16,128,128]{2,1,0:T(8,128)(2,1)S(1)} async-done(((bf16[16,128,128]{2,1,0:T(8,128)(2,1)}), bf16[16,128,128]{2,1,0:T(8,128)(2,1)S(1)}, u32[]{:S(2)}, u32[]{:S(2)}) %all-to-all-start) | async-done | bytes 524320 | tf_op jit(solution)/shard_map/all_to_all | solution.py:340
  81.6 6.7 %second.1 = bf16[16,16,128]{2,1,0:T(8,128)(2,1)} custom-call(bf16[16,128,128]{2,1,0:T(8,128)(2,1)S(1)} %all-to-all-done.half_ref, s32[1,128]{1,0:T(1,128)S(1)} %reshape.36.ids_ref, bf16[16,256,256]{2,1,0:T(8,128)(2,1)} %constant.11.clone.table_any, bf16[128,1024]{1,0:T(8,128)(2,1)} %constant.12.clone.place_any), custom_call_target="tpu_custom_call" | custom-call | tf_op jit(solution)/shard_map/second/pallas_call | solution.py:329
  88.4 3.7 %all-to-all-start.2 = ((bf16[16,16,128]{2,1,0:T(8,128)(2,1)}), bf16[16,16,128]{2,1,0:T(8,128)(2,1)S(1)}, u32[]{:S(2)}, u32[]{:S(2)}) async-start(bf16[16,16,128]{2,1,0:T(8,128)(2,1)} %second.1), calls=%async_computation.2 | async-start | bytes 131072 | tf_op jit(solution)/shard_map/all_to_all | solution.py:340
  92.1 7.2 %all-to-all-done.2 = bf16[16,16,128]{2,1,0:T(8,128)(2,1)S(1)} async-done(((bf16[16,16,128]{2,1,0:T(8,128)(2,1)}), bf16[16,16,128]{2,1,0:T(8,128)(2,1)S(1)}, u32[]{:S(2)}, u32[]{:S(2)}) %all-to-all-start.2) | async-done | bytes 65568 | tf_op jit(solution)/shard_map/all_to_all | solution.py:340
  99.2 6.9 %visit.1 = (f32[128,128]{1,0:T(8,128)}, bf16[256,128]{1,0:T(8,128)(2,1)}) custom-call(bf16[256,128]{1,0:T(8,128)(2,1)S(1)} %bitcast.17, bf16[128,256]{1,0:T(8,128)(2,1)S(1)} %get-tuple-element.15.pick_ref, bf16[256,128]{1,0:T(8,128)(2,1)S(1)} %get-tuple-element.16.put_ref, f32[128,128]{1,0:T(8,128)S(1)} %get-tuple-element.17.live_ref, ...), custom_call_target="tpu_custom_call" | custom-call | tf_op jit(solution)/shard_map/visit/pallas_call | solution.py:329
  106.1 3.7 %all-to-all-start.3 = ((bf16[16,16,128]{2,1,0:T(8,128)(2,1)}), bf16[16,16,128]{2,1,0:T(8,128)(2,1)S(1)}, u32[]{:S(2)}, u32[]{:S(2)}) async-start(bf16[16,16,128]{2,1,0:T(8,128)(2,1)} %bitcast.22), calls=%async_computation.3 | async-start | bytes 131072 | tf_op jit(solution)/shard_map/all_to_all | solution.py:340
  109.9 0.1 copy.24
  109.9 0.1 reshape.43.target_ref
  110.0 7.6 %all-to-all-done.3 = bf16[16,16,128]{2,1,0:T(8,128)(2,1)S(1)} async-done(((bf16[16,16,128]{2,1,0:T(8,128)(2,1)}), bf16[16,16,128]{2,1,0:T(8,128)(2,1)S(1)}, u32[]{:S(2)}, u32[]{:S(2)}) %all-to-all-start.3) | async-done | bytes 65568 | tf_op jit(solution)/shard_map/all_to_all | solution.py:340
  117.6 1.2 %dirty.1 = f32[2048,128]{1,0:T(8,128)} custom-call(bf16[256,128]{1,0:T(8,128)(2,1)S(1)} %bitcast.16, s32[1,256]{1,0:T(1,128)S(1)} %reshape.43.target_ref), custom_call_target="tpu_custom_call" | custom-call | tf_op jit(solution)/shard_map/dirty/pallas_call | solution.py:329
  (6 shorter events, 0.0 us)
Async XLA Ops:
  1.6 51.6 %collective-permute-start = (bf16[128,512]{1,0:T(8,128)(2,1)S(1)}, bf16[128,512]{1,0:T(8,128)(2,1)S(1)}, u32[]{:S(2)}, u32[]{:S(2)}) collective-permute-start(bf16[128,512]{1,0:T(8,128)(2,1)S(1)} %get-tuple-element.21), channel_id=1, source_target_pairs={{0,16},{16,32},{32,48},{48,64},{64,80},{80,96},{96,112},{112,128},... | collective-permute-start | bytes 393224 | tf_op jit(solution)/shard_map/ppermute | solution.py:355
  8.2 45.0 %collective-permute-start.1 = (bf16[128,512]{1,0:T(8,128)(2,1)S(1)}, bf16[128,512]{1,0:T(8,128)(2,1)S(1)}, u32[]{:S(2)}, u32[]{:S(2)}) collective-permute-start(bf16[128,512]{1,0:T(8,128)(2,1)S(1)} %get-tuple-element.20), channel_id=1, source_target_pairs={{16,0},{32,16},{48,32},{64,48},{80,64},{96,80},{112,96},{128,112},... | collective-permute-start | bytes 393224 | tf_op jit(solution)/shard_map/ppermute | solution.py:356
  13.7 46.6 %all-to-all-start.1 = ((s32[16,1,8]{2,1,0:T(1,128)}), s32[16,1,8]{2,1,0:T(1,128)S(1)}, u32[]{:S(2)}, u32[]{:S(2)}) async-start(s32[16,1,8]{2,1,0:T(1,128)} %bitcast.23), calls=%async_computation.1 | async-start | bytes 16384 | tf_op jit(solution)/shard_map/all_to_all | solution.py:340
  54.7 44.5 %copy-start = (f32[1,64,2,128]{3,2,1,0:T(2,128)S(1)}, f32[1,64,2,128]{3,2,1,0:T(2,128)}, u32[]{:S(2)}) copy-start(f32[1,64,2,128]{3,2,1,0:T(2,128)} %param.13) | copy-start | bytes 196612
  60.4 21.2 %all-to-all-start = ((bf16[16,128,128]{2,1,0:T(8,128)(2,1)}), bf16[16,128,128]{2,1,0:T(8,128)(2,1)S(1)}, u32[]{:S(2)}, u32[]{:S(2)}) async-start(bf16[16,128,128]{2,1,0:T(8,128)(2,1)} %first.1), calls=%async_computation | async-start | bytes 1048576 | tf_op jit(solution)/shard_map/all_to_all | solution.py:340
  88.4 10.9 %all-to-all-start.2 = ((bf16[16,16,128]{2,1,0:T(8,128)(2,1)}), bf16[16,16,128]{2,1,0:T(8,128)(2,1)S(1)}, u32[]{:S(2)}, u32[]{:S(2)}) async-start(bf16[16,16,128]{2,1,0:T(8,128)(2,1)} %second.1), calls=%async_computation.2 | async-start | bytes 131072 | tf_op jit(solution)/shard_map/all_to_all | solution.py:340
  106.1 11.5 %all-to-all-start.3 = ((bf16[16,16,128]{2,1,0:T(8,128)(2,1)}), bf16[16,16,128]{2,1,0:T(8,128)(2,1)S(1)}, u32[]{:S(2)}, u32[]{:S(2)}) async-start(bf16[16,16,128]{2,1,0:T(8,128)(2,1)} %bitcast.22), calls=%async_computation.3 | async-start | bytes 131072 | tf_op jit(solution)/shard_map/all_to_all | solution.py:340

commit v2 on v1

v2 whole, which is shorter than its diff:
```python
import math

import jax
import jax.numpy as jnp
import numpy as np
from jax import lax
from jax.experimental import pallas as pl
from jax.experimental.pallas import tpu as pltpu
from jax.sharding import PartitionSpec as P

GRID = 2048
HALO = 512
RADIX = 16
LANES = GRID // RADIX
GROUP_AXES = ("bl", "pol")
F32 = jnp.float32
BF16 = jnp.bfloat16


def spin(re, im, k, n):
    k = k % n
    c, s = math.cos(2 * math.pi * k / n), math.sin(2 * math.pi * k / n)
    if k == 0:
        return re, im
    if 4 * k == n:
        return im, -re
    if im is None:
        return re * np.float32(c), re * np.float32(-s)
    if 8 * k == n:
        h = np.float32(math.sqrt(0.5))
        return (re + im) * h, (im - re) * h
    if 8 * k == 3 * n:
        h = np.float32(math.sqrt(0.5))
        return (im - re) * h, (re + im) * -h
    return re * np.float32(c) + im * np.float32(s), im * np.float32(c) - re * np.float32(s)


def plus(a, b):
    return b if a is None else a if b is None else a + b


def minus(a, b):
    return a if b is None else -b if a is None else a - b


def real_dft(x):
    n = len(x)
    if n == 1:
        return [(x[0], None)]
    if n == 2:
        return [(x[0] + x[1], None), (x[0] - x[1], None)]
    even, odd = real_dft(x[0::2]), real_dft(x[1::2])
    out = [None] * (n // 2 + 1)
    for k in range(n // 4 + 1):
        (er, ei), (orr, oi) = even[k], odd[k]
        if 4 * k == n:
            tr, ti = None, (None if orr is None else -orr)
        else:
            tr, ti = spin(orr, oi, k, n)
        out[k] = (plus(er, tr), plus(ei, ti))
        if n // 2 - k != k:
            low = minus(ei, ti)
            out[n // 2 - k] = (minus(er, tr), None if low is None else minus(None, low))
    return out


def first_table():
    half = RADIX // 2
    p, s, u0 = np.meshgrid(
        np.arange(half), np.arange(2), np.arange(GRID // 2 // RADIX), indexing="ij"
    )
    u1 = np.where(s == 0, p, np.where(p == 0, half, RADIX - p))
    u = RADIX * u0 + u1
    x0 = np.arange(LANES)
    angle = 2 * np.pi * ((u[..., None] * x0) % GRID) / GRID
    c, n = np.cos(angle) / math.sqrt(GRID), np.sin(angle) / math.sqrt(GRID)
    first = (p == 0)[..., None]
    side = (s == 0)[..., None]
    sign = np.where(side, 1.0, -1.0)
    rr = np.where(first, np.where(side, c, 0.0), c)
    ri = np.where(first, np.where(side, 0.0, c), sign * n)
    ir = np.where(first, np.where(side, -n, 0.0), -n)
    ii = np.where(first, np.where(side, 0.0, -n), sign * c)
    real = np.concatenate([rr, ri], axis=-1)
    imag = np.concatenate([ir, ii], axis=-1)
    both = np.stack([real, imag], axis=1)
    return both.reshape(half, 2 * GRID // RADIX, 2 * LANES).astype(np.float32).astype(BF16)


def turn_table():
    angle = 2 * np.pi * (np.outer(np.arange(LANES), np.arange(LANES)) % LANES) / LANES
    return np.stack([np.cos(angle), np.sin(angle)]).astype(np.float32)


def mix_table(group):
    y = np.arange(group * LANES).reshape(group, LANES, 1)
    angle = 2 * np.pi * ((y * np.arange(RADIX)) % GRID) / GRID
    c, n = np.cos(angle) / math.sqrt(GRID), np.sin(angle) / math.sqrt(GRID)
    top = np.concatenate([c, -n], axis=2)
    low = np.concatenate([n, c], axis=2)
    both = np.concatenate([top, low], axis=1)
    return np.tile(both, (1, 1, LANES // (2 * RADIX))).astype(np.float32).astype(BF16)


def dot(a, b, dims=((1,), (0,))):
    return lax.dot_general(a, b, (dims, ((), ())), preferred_element_type=F32)


def iota(shape, dim):
    return lax.broadcasted_iota(jnp.int32, shape, dim)


def plan_body(
    owner_ref, count_ref, sky_any, pattern_any, table_any,
    put_ref, live_ref, sky_ref, pattern_ref, table_ref, sems,
):
    copies = [
        pltpu.make_async_copy(source, target, sems.at[i])
        for i, (source, target) in enumerate(
            [(sky_any, sky_ref), (pattern_any, pattern_ref), (table_any, table_ref)]
        )
    ]
    for copy in copies:
        copy.start()
    n = owner_ref.shape[1]
    wide, rows = put_ref.shape
    cap = wide // (2 * GRID // LANES)
    owner_row = owner_ref[...].astype(F32)
    count_row = count_ref[...].astype(F32)
    eye = iota((n, n), 0) == iota((n, n), 1)
    owner_col = jnp.sum(jnp.where(eye, owner_row, 0.0), axis=1, keepdims=True)
    after = jnp.where((owner_col == owner_row) & (iota((n, n), 1) < iota((n, n), 0)), 1.0, 0.0)
    slot_col = jnp.sum(after, axis=1, keepdims=True)
    target_col = owner_col * float(2 * cap) + slot_col
    spread = jnp.where(iota((n, rows), 1) // 2 == iota((n, rows), 0), 1.0, 0.0)
    row = jnp.sum(spread * target_col, axis=0, keepdims=True)
    row = row + (iota((1, rows), 1) % 2 * cap).astype(F32)
    put_ref[...] = jnp.where(iota((wide, rows), 0).astype(F32) == row, 1.0, 0.0).astype(BF16)
    double = jnp.where(iota((rows, n), 0) // 2 == iota((rows, n), 1), 1.0, 0.0)
    count = jnp.sum(double * count_row, axis=1, keepdims=True)
    live_ref[...] = jnp.where(iota(live_ref.shape, 1).astype(F32) < count, 1.0, 0.0)
    for copy in copies:
        copy.wait()


def sky_body(
    me_ref, asked_ref, low_ref, sky_ref, high_ref, pattern_ref, table_ref, turn_any, mix_any,
    out_any, mid_ref, half_ref, left_ref, turn_ref, mix_ref, wide_ref, out_ref, asked_smem, sems,
):
    ids = pltpu.make_async_copy(asked_ref, asked_smem, sems.at[0])
    turn = pltpu.make_async_copy(turn_any, turn_ref, sems.at[1])
    mix = pltpu.make_async_copy(mix_any.at[me_ref[0]], mix_ref, sems.at[2])
    for copy in (ids, turn, mix):
        copy.start()
    rows = sky_ref.shape[0]
    block = 16
    for start in range(0, rows, block):
        at = slice(start, start + block)
        parts = []
        for x1 in range(RADIX):
            lo = x1 * LANES
            if lo < HALO:
                sky = low_ref[at, lo : lo + LANES]
            elif lo < GRID - HALO:
                sky = sky_ref[at, lo - HALO : lo - HALO + LANES]
            else:
                sky = high_ref[at, lo - GRID + HALO : lo - GRID + HALO + LANES]
            seen = pattern_ref[at, lo : lo + LANES].astype(F32) * sky.astype(F32)
            parts.append(seen.astype(BF16).astype(F32))
        out = real_dft(parts)
        mid_ref[0, at, :LANES] = out[0][0].astype(BF16)
        mid_ref[0, at, LANES:] = out[RADIX // 2][0].astype(BF16)
        for p in range(1, RADIX // 2):
            mid_ref[p, at, :LANES] = out[p][0].astype(BF16)
            mid_ref[p, at, LANES:] = out[p][1].astype(BF16)
    per = GRID // 2 // RADIX
    for p in range(RADIX // 2):
        half = dot(table_ref[p], mid_ref[p], ((1,), (1,))).astype(BF16).astype(F32)
        for c in range(2):
            for s in range(2):
                i = p if s == 0 else (8 - p) % 8
                first = (2 * c + s) * per
                half_ref[pl.ds(16 * s + 8 * c + i, per, stride=32), :] = half[first : first + per]
    mix.wait()
    quarter = LANES // 4
    for q in range(4):
        held = mix_ref[...].astype(F32)
        lane = iota(held.shape, 1) // quarter == q
        wide_ref[2 * LANES * q : 2 * LANES * (q + 1), :] = jnp.where(lane, held, 0.0).astype(BF16)
    ids.wait()
    turn.wait()
    group, vis = asked_ref.shape
    steps = vis // 8

    def step(n, carry):
        dest, first = n // steps, n % steps * 8
        both = []
        for r in range(8):
            tile = asked_smem[dest, first + r]
            at = pl.multiple_of(tile // LANES * 16, 16)
            v0 = tile % LANES
            re, im = half_ref[pl.ds(at, 8), :], half_ref[pl.ds(at + 8, 8), :]
            c, s = turn_ref[0, pl.ds(v0, 1), :], turn_ref[1, pl.ds(v0, 1), :]
            both.append((re * c + im * s, im * c - re * s))
        at = pl.ds(pl.multiple_of(n * 16, 16), 16)
        for q in range(4):
            for part in range(2):
                lo = (2 * q + part) * LANES
                pair = jnp.concatenate([both[q][part], both[q + 4][part]], axis=0)
                left_ref[at, lo : lo + LANES] = pair.astype(BF16)
        return carry

    lax.fori_loop(0, group * steps, step, 0, unroll=4)
    copies = []
    chunk = 256
    for i in range(group * vis * 2 // chunk):
        at = pl.ds(i * chunk, chunk)
        out_ref[at, :] = dot(left_ref[at, :], wide_ref[...]).astype(BF16)
        copies.append(pltpu.make_async_copy(out_ref.at[at], out_any.at[at], sems.at[3 + i]))
        copies[-1].start()
    for copy in copies:
        copy.wait()


def target_body(me_ref, asked_ref, kernel_any, target_ref, kernel_ref, sem):
    copy = pltpu.make_async_copy(kernel_any, kernel_ref, sem)
    copy.start()
    group, n = asked_ref.shape
    wide = target_ref.shape[1]
    cap = wide // (2 * group)
    asked = asked_ref[...]
    each = LANES * 8
    mine = asked // each == me_ref[0]
    local = (asked % each).astype(F32)
    before = jnp.where(iota((n, n), 0) < iota((n, n), 1), 1.0, 0.0).astype(BF16)
    slot = dot(jnp.where(mine, 1.0, 0.0).astype(BF16), before)
    lane = iota((group, wide), 1)
    found = jnp.zeros((group, wide), F32)
    for k in range(cap):
        hit = jnp.where(mine & (slot == float(k)), local + 1.0, 0.0)
        found = jnp.where(lane % cap == k, jnp.sum(hit, axis=1, keepdims=True), found)
    found = 2.0 * (found - 1.0) + (lane // cap % 2).astype(F32)
    own = lane // (2 * cap) == iota((group, wide), 0)
    target_ref[...] = jnp.sum(jnp.where(own, found, 0.0), axis=0, keepdims=True).astype(jnp.int32)
    copy.wait()


def swap_blocks(x):
    sub, block = iota(x.shape, 0), iota(x.shape, 1) // RADIX
    for bit in (1, 2, 4):
        up = pltpu.roll(pltpu.roll(x, 8 - bit, 0), RADIX * bit, 1)
        down = pltpu.roll(pltpu.roll(x, bit, 0), LANES - RADIX * bit, 1)
        s, b = sub & bit, block & bit
        x = jnp.where(s == b, x, jnp.where(s == 0, up, down))
    return x


def visit_body(tiles_ref, put_ref, live_ref, seen_ref, kernel_ref, res_ref, out_ref):
    cells = kernel_ref.shape[1]
    rows = seen_ref.shape[0]
    of = iota((8, cells), 0) // 2

    def left(own, h):
        return jnp.concatenate(
            [jnp.where(of == 2 * h + q, own, 0.0) for q in range(2)], axis=1
        ).astype(BF16)

    blocks = range(rows // 8)
    guesses = []
    for g in blocks:
        at = slice(8 * g, 8 * g + 8)
        total = tiles_ref[0, at].astype(F32)
        for source in range(1, tiles_ref.shape[0]):
            total = total + tiles_ref[source, at].astype(F32)
        own = swap_blocks(total.astype(BF16).astype(F32))
        guess = None
        for h in range(2):
            first = (4 * g + 2 * h) * cells
            right = jnp.concatenate(
                [kernel_ref[first : first + cells], kernel_ref[first + cells : first + 2 * cells]],
                axis=1,
            )
            guess = plus(guess, dot(left(own, h), right, ((1,), (1,))))
        guesses.append(guess)
    res = jnp.where(live_ref[...] > 0.0, seen_ref[...] - jnp.concatenate(guesses, axis=0), 0.0)
    res_ref[...] = res
    terms = []
    for g in blocks:
        own = res[8 * g : 8 * g + 8]
        term = None
        for h in range(2):
            first = (4 * g + 2 * h) * cells
            term = plus(term, dot(left(own, h), kernel_ref[first : first + 2 * cells]))
        terms.append(term)
    term = jnp.concatenate(terms, axis=0).astype(BF16)
    out_ref[...] = dot(put_ref[...], term).astype(BF16)


def dirty_body(term_ref, target_ref, out_any, out_ref, sems):
    rows = out_ref.shape[0]
    step = rows // sems.shape[0]
    target = target_ref[...]
    term = term_ref[...]
    copies = []
    for i in range(sems.shape[0]):
        at = pl.ds(i * step, step)
        hot = jnp.where(iota((step, target.shape[1]), 0) + i * step == target, 1.0, 0.0)
        out_ref[at, :] = dot(hot.astype(BF16), term)
        copies.append(pltpu.make_async_copy(out_ref.at[at], out_any.at[at], sems.at[i]))
        copies[-1].start()
    for copy in copies:
        copy.wait()


FAST = pltpu.VMEM
ANY = pl.ANY


def call(body, name, outs, args, scratch=()):
    shapes = [
        pltpu.VMEM(s, d) if space is FAST else jax.ShapeDtypeStruct(s, d) for s, d, space in outs
    ]
    spec = lambda space: pl.BlockSpec(memory_space=pltpu.VMEM if space is None else space)
    return pl.pallas_call(
        body,
        out_shape=shapes,
        in_specs=[spec(space) for _, space in args],
        out_specs=[spec(space) for _, _, space in outs],
        scratch_shapes=list(scratch),
        name=name,
    )(*[pltpu.with_memory_space_constraint(a, FAST) if space is FAST else a for a, space in args])


def exchange(block):
    return lax.all_to_all(block, GROUP_AXES, split_axis=0, concat_axis=0, tiled=True)


def on_device(sky_model, beam_pattern, kernels, observed, tile_owner, tile_local, vis_count):
    group = lax.axis_size(GROUP_AXES)
    rows, strip = sky_model.shape
    vis, cells = kernels.shape[1], kernels.shape[3]
    cap = max(2, 2 * vis // group)
    u_rows = GRID // 2 // group
    tiles_dev = u_rows // 8 * (GRID // 16)
    sem = pltpu.SemaphoreType.DMA
    me = lax.axis_index(GROUP_AXES).astype(jnp.int32).reshape(1)

    numbers = tile_owner[:, :, 0] * tiles_dev + tile_local
    asked = exchange(jnp.broadcast_to(numbers, (group, vis)))

    count = lax.axis_size("beam")
    forward = [(i, i + 1) for i in range(count - 1)]
    backward = [(target, source) for source, target in forward]
    low = lax.ppermute(sky_model[:, strip - HALO :], "beam", forward)
    high = lax.ppermute(sky_model[:, :HALO], "beam", backward)

    table = first_table()
    put, live, sky_fast, pattern_fast, table_fast = call(
        plan_body,
        "plan",
        [
            ((2 * group * cap, 2 * vis), BF16, FAST),
            ((2 * vis, cells), F32, FAST),
            ((rows, strip), BF16, FAST),
            ((rows, GRID), BF16, FAST),
            (table.shape, BF16, FAST),
        ],
        [
            (tile_owner[:, :, 0], None),
            (vis_count, None),
            (sky_model, ANY),
            (beam_pattern[0], ANY),
            (table, ANY),
        ],
        [sem((3,))],
    )
    turn, mix = turn_table(), mix_table(group)
    (partial,) = call(
        sky_body,
        "sky",
        [((group * 2 * vis, cells), BF16, ANY)],
        [
            (me, pltpu.SMEM),
            (asked, FAST),
            (low, FAST),
            (sky_fast, FAST),
            (high, FAST),
            (pattern_fast, FAST),
            (table_fast, FAST),
            (turn, ANY),
            (mix, ANY),
        ],
        [
            pltpu.VMEM((RADIX // 2, rows, 2 * LANES), BF16),
            pltpu.VMEM((GRID, LANES), F32),
            pltpu.VMEM((group * 2 * vis, 8 * LANES), BF16),
            pltpu.VMEM(turn.shape, F32),
            pltpu.VMEM(mix.shape[1:], BF16),
            pltpu.VMEM((8 * LANES, LANES), BF16),
            pltpu.VMEM((group * 2 * vis, cells), BF16),
            pltpu.SMEM((group, vis), jnp.int32),
            sem((3 + group * 2 * vis // 256,)),
        ],
    )
    tiles = exchange(partial.reshape(group, 2 * vis, cells))
    target, kernels_fast = call(
        target_body,
        "target",
        [((1, 2 * group * cap), jnp.int32, FAST), ((vis * cells, cells), BF16, FAST)],
        [(me, pltpu.SMEM), (asked, FAST), (kernels.reshape(vis * cells, cells), ANY)],
        [sem],
    )
    residual, terms = call(
        visit_body,
        "visit",
        [((2 * vis, cells), F32, None), ((2 * group * cap, cells), BF16, None)],
        [
            (tiles, FAST),
            (put, FAST),
            (live, FAST),
            (observed.reshape(2 * vis, cells), FAST),
            (kernels_fast, FAST),
        ],
    )
    arrived = exchange(terms.reshape(group, 2 * cap, cells))
    (dirty,) = call(
        dirty_body,
        "dirty",
        [((2 * tiles_dev, cells), F32, ANY)],
        [(arrived.reshape(2 * group * cap, cells), FAST), (target, FAST)],
        [pltpu.VMEM((2 * tiles_dev, cells), F32), sem((8,))],
    )
    return residual.reshape(1, vis, 2, cells), dirty.reshape(1, tiles_dev, 2, cells)


def solution(mesh):
    placed = (
        P(("tile", "bl", "pol"), "beam"),
        P(("tile", "beam"), ("bl", "pol"), None),
        P(("tile", "beam"), ("bl", "pol"), None, None),
        P(("tile", "beam"), ("bl", "pol"), None, None),
        P(("tile", "beam"), ("bl", "pol"), None),
        P(("tile", "beam"), ("bl", "pol")),
        P(("tile", "beam"), ("bl", "pol")),
    )
    return jax.shard_map(
        on_device,
        mesh=mesh,
        in_specs=placed,
        out_specs=(
            P(("tile", "beam"), ("bl", "pol"), None, None),
            P(("tile", "beam"), ("bl", "pol"), None, None),
        ),
        check_vma=False,
    )
```

time: 119 us -> 109 us (0.916)
  waiting for transfers between devices: 36.3 us -> 20.5 us
  blocking collectives: 0 us -> 10.8 us
  starting transfers between devices: 58.7 us -> 54.8 us
  local copies, waits for them, and re-layouts: 3.17 us -> 1.6 us
    all_to_all x4 -> x2, waiting for transfers between devices: 36.3 us -> 20.5 us  [exchange(): lax.all_to_all(block, GROUP_AXES, split_axis=0, concat_axis=0, tiled=True)]
    all_to_all x0 -> x1, blocking collectives: none -> 10.8 us  [exchange(): lax.all_to_all(block, GROUP_AXES, split_axis=0, concat_axis=0, tiled=True)]
    all_to_all x4 -> x2, starting transfers between devices: 50.9 us -> 46.3 us  [exchange(): lax.all_to_all(block, GROUP_AXES, split_axis=0, concat_axis=0, tiled=True)]
    squeeze x1 -> x0, local copies, waits for them, and re-layouts: 1.36 us -> none  [on_device(): tile_owner[0]]
  transfers between devices with their start and end apart: 6 -> 4, of which waited for: 4 -> 2; matrix products, arithmetic and copies ran while one was open for 2% -> 1% of each run, Pallas kernels for 4% -> 3%
where the time goes in v2:
time: 109 us
  starting transfers between devices  54.8 us (50%)
  waiting for transfers between devices  20.5 us (19%)
  Pallas kernels  19.5 us (18%)
  blocking collectives  10.8 us (10%)
  local copies, waits for them, and re-layouts  1.6 us (1%)
    all_to_all x2, starting transfers between devices, exchange(): lax.all_to_all(block, GROUP_AXES, split_axis=0, concat_axis=0, tiled=True)  46.3 us
    all_to_all x2, waiting for transfers between devices, exchange(): lax.all_to_all(block, GROUP_AXES, split_axis=0, concat_axis=0, tiled=True)  20.5 us
    pallas_call x5, Pallas kernels, call(): pl.pallas_call(body, out_shape=shapes, in_specs=[spec(space) for _, space...  19.5 us
    all_to_all x1, blocking collectives, exchange(): lax.all_to_all(block, GROUP_AXES, split_axis=0, concat_axis=0, tiled=True)  10.8 us
    ppermute x1, starting transfers between devices, on_device(): low = lax.ppermute(sky_model[:, strip - HALO:], 'beam', forward)  7.21 us
  transfers between devices with their start and end apart: 4, of which 2 were waited for; matrix products, arithmetic and copies ran while one was open for 1% of the time, Pallas kernels for 3%

profile of v2, /device:TPU:65, one launch (start us, length us, event | category | flops | bytes accessed | tf_op | source)
XLA Modules:
  0.0 108.6 jit_solution(8161639592012529645)
XLA Ops:
  0.6 1.0 fusion
  1.6 1.3 %collective-permute-start.1 = (bf16[128,512]{1,0:T(8,128)(2,1)S(1)}, bf16[128,512]{1,0:T(8,128)(2,1)S(1)}, u32[]{:S(2)}, u32[]{:S(2)}) collective-permute-start(bf16[128,512]{1,0:T(8,128)(2,1)S(1)} %get-tuple-element.20), channel_id=1, source_target_pairs={{16,0},{32,16},{48,32},{64,48},{80,64},{96,80},{112,96},{128,112},... | collective-permute-start | bytes 393224 | tf_op jit(solution)/shard_map/ppermute | solution.py:355
  2.9 7.2 %collective-permute-start = (bf16[128,512]{1,0:T(8,128)(2,1)S(1)}, bf16[128,512]{1,0:T(8,128)(2,1)S(1)}, u32[]{:S(2)}, u32[]{:S(2)}) collective-permute-start(bf16[128,512]{1,0:T(8,128)(2,1)S(1)} %get-tuple-element.21), channel_id=1, source_target_pairs={{0,16},{16,32},{32,48},{48,64},{64,80},{80,96},{96,112},{112,128},... | collective-permute-start | bytes 393224 | tf_op jit(solution)/shard_map/ppermute | solution.py:354
  10.2 0.7 add_bitcast_fusion
  10.8 0.6 broadcast_in_dim.2
  11.4 42.1 %all-to-all-start = ((s32[16,1,64]{2,1,0:T(1,128)}), s32[16,1,64]{2,1,0:T(1,128)S(1)}, u32[]{:S(2)}, u32[]{:S(2)}) async-start(s32[16,1,64]{2,1,0:T(1,128)} %broadcast_in_dim.2), calls=%async_computation | async-start | bytes 16384 | tf_op jit(solution)/shard_map/all_to_all | solution.py:335
  53.5 2.2 %plan.1 = (bf16[256,128]{1,0:T(8,128)(2,1)S(1)}, f32[128,128]{1,0:T(8,128)S(1)}, bf16[128,1024]{1,0:T(8,128)(2,1)S(1)}, bf16[128,2048]{1,0:T(8,128)(2,1)S(1)}, bf16[8,256,256]{2,1,0:T(8,128)(2,1)S(1)}) custom-call(s32[1,64]{1,0:T(1,128)} %bitcast.23, s32[1,64]{1,0:T(1,128)} %count_ref.1, bf16[128,1024]{1,0:T(8,128)(2,1)} %sky_any.1, ...), custom_call_target="tpu_custom_call" | custom-call | tf_op jit(solution)/shard_map/plan/pallas_call | solution.py:324
  55.7 4.9 %all-to-all-done = s32[16,1,64]{2,1,0:T(1,128)S(1)} async-done(((s32[16,1,64]{2,1,0:T(1,128)}), s32[16,1,64]{2,1,0:T(1,128)S(1)}, u32[]{:S(2)}, u32[]{:S(2)}) %all-to-all-start) | async-done | bytes 4128 | tf_op jit(solution)/shard_map/all_to_all | solution.py:335
  60.6 0.0 collective-permute-done.1.high_ref
  60.6 0.0 collective-permute-done.low_ref
  60.6 12.4 %sky.1 = bf16[2048,128]{1,0:T(8,128)(2,1)} custom-call(s32[1]{0:T(128)} %bitcast.me_ref, s32[16,64]{1,0:T(8,128)S(1)} %bitcast.15, bf16[128,512]{1,0:T(8,128)(2,1)S(1)} %collective-permute-done.low_ref, bf16[128,1024]{1,0:T(8,128)(2,1)S(1)} %get-tuple-element.11.sky_ref, bf16[128,512]{1,0:T(8,128)(2,1)S(1)} %collective-permute-done.1.high_ref, ...), custom_call_target="tpu_custom_call" | custom-call | tf_op jit(solution)/shard_map/sky/pallas_call | solution.py:324
  73.0 0.0 copy-start
  73.0 4.2 %all-to-all-start.1 = ((bf16[16,128,128]{2,1,0:T(8,128)(2,1)}), bf16[16,128,128]{2,1,0:T(8,128)(2,1)S(1)}, u32[]{:S(2)}, u32[]{:S(2)}) async-start(bf16[16,128,128]{2,1,0:T(8,128)(2,1)} %bitcast.19), calls=%async_computation.1 | async-start | bytes 1048576 | tf_op jit(solution)/shard_map/all_to_all | solution.py:335
  77.2 1.6 %target.1 = (s32[1,256]{1,0:T(1,128)S(1)}, bf16[8192,128]{1,0:T(8,128)(2,1)S(1)}) custom-call(s32[1]{0:T(128)} %bitcast.me_ref, s32[16,64]{1,0:T(8,128)S(1)} %bitcast.16, bf16[8192,128]{1,0:T(8,128)(2,1)} %bitcast.18), custom_call_target="tpu_custom_call" | custom-call | tf_op jit(solution)/shard_map/target/pallas_call | solution.py:324
  78.8 15.6 %all-to-all-done.1.tiles_ref = bf16[16,128,128]{2,1,0:T(8,128)(2,1)S(1)} async-done(((bf16[16,128,128]{2,1,0:T(8,128)(2,1)}), bf16[16,128,128]{2,1,0:T(8,128)(2,1)S(1)}, u32[]{:S(2)}, u32[]{:S(2)}) %all-to-all-start.1) | async-done | bytes 524320 | tf_op jit(solution)/shard_map/all_to_all | solution.py:335
  94.4 0.0 copy-done
  94.4 2.1 %visit.1 = (f32[128,128]{1,0:T(8,128)}, bf16[256,128]{1,0:T(8,128)(2,1)}) custom-call(bf16[16,128,128]{2,1,0:T(8,128)(2,1)S(1)} %all-to-all-done.1.tiles_ref, bf16[256,128]{1,0:T(8,128)(2,1)S(1)} %get-tuple-element.14.put_ref, f32[128,128]{1,0:T(8,128)S(1)} %get-tuple-element.15.live_ref, f32[128,128]{1,0:T(8,128)S(1)} %bitcast.17, ...), custom_call_target="tpu_custom_call" | custom-call | tf_op jit(solution)/shard_map/visit/pallas_call | solution.py:324
  96.6 10.8 %all_to_all.18 = bf16[16,16,128]{2,1,0:T(8,128)(2,1)S(1)} all-to-all(bf16[16,16,128]{2,1,0:T(8,128)(2,1)} %bitcast.22), channel_id=1, replica_groups=mesh['tile'=2,'beam'=16,'bl'=8,'pol'=2] {'bl','pol'}, dimensions={0} | all-to-all | bytes 131072 | tf_op jit(solution)/shard_map/all_to_all | solution.py:335
  107.4 1.2 %dirty.1 = f32[2048,128]{1,0:T(8,128)} custom-call(bf16[256,128]{1,0:T(8,128)(2,1)S(1)} %bitcast.14, s32[1,256]{1,0:T(1,128)S(1)} %get-tuple-element.19.target_ref), custom_call_target="tpu_custom_call" | custom-call | tf_op jit(solution)/shard_map/dirty/pallas_call | solution.py:324
Async XLA Ops:
  1.6 59.0 %collective-permute-start.1 = (bf16[128,512]{1,0:T(8,128)(2,1)S(1)}, bf16[128,512]{1,0:T(8,128)(2,1)S(1)}, u32[]{:S(2)}, u32[]{:S(2)}) collective-permute-start(bf16[128,512]{1,0:T(8,128)(2,1)S(1)} %get-tuple-element.20), channel_id=1, source_target_pairs={{16,0},{32,16},{48,32},{64,48},{80,64},{96,80},{112,96},{128,112},... | collective-permute-start | bytes 393224 | tf_op jit(solution)/shard_map/ppermute | solution.py:355
  2.9 57.7 %collective-permute-start = (bf16[128,512]{1,0:T(8,128)(2,1)S(1)}, bf16[128,512]{1,0:T(8,128)(2,1)S(1)}, u32[]{:S(2)}, u32[]{:S(2)}) collective-permute-start(bf16[128,512]{1,0:T(8,128)(2,1)S(1)} %get-tuple-element.21), channel_id=1, source_target_pairs={{0,16},{16,32},{32,48},{48,64},{64,80},{80,96},{96,112},{112,128},... | collective-permute-start | bytes 393224 | tf_op jit(solution)/shard_map/ppermute | solution.py:354
  11.4 49.2 %all-to-all-start = ((s32[16,1,64]{2,1,0:T(1,128)}), s32[16,1,64]{2,1,0:T(1,128)S(1)}, u32[]{:S(2)}, u32[]{:S(2)}) async-start(s32[16,1,64]{2,1,0:T(1,128)} %broadcast_in_dim.2), calls=%async_computation | async-start | bytes 16384 | tf_op jit(solution)/shard_map/all_to_all | solution.py:335
  73.0 21.4 %copy-start = (f32[1,64,2,128]{3,2,1,0:T(2,128)S(1)}, f32[1,64,2,128]{3,2,1,0:T(2,128)}, u32[]{:S(2)}) copy-start(f32[1,64,2,128]{3,2,1,0:T(2,128)} %param.13) | copy-start | bytes 196612
  73.0 21.4 %all-to-all-start.1 = ((bf16[16,128,128]{2,1,0:T(8,128)(2,1)}), bf16[16,128,128]{2,1,0:T(8,128)(2,1)S(1)}, u32[]{:S(2)}, u32[]{:S(2)}) async-start(bf16[16,128,128]{2,1,0:T(8,128)(2,1)} %bitcast.19), calls=%async_computation.1 | async-start | bytes 1048576 | tf_op jit(solution)/shard_map/all_to_all | solution.py:335

commit v3 on v2

--- a/solution.py
+++ b/solution.py
@@ -108,6 +108,18 @@
 
 def iota(shape, dim):
     return lax.broadcasted_iota(jnp.int32, shape, dim)
+
+
+def ask_body(owner_ref, local_ref, sky_any, asked_ref, first_ref, last_ref, sems):
+    strip, width = sky_any.shape[1], first_ref.shape[1]
+    first = pltpu.make_async_copy(sky_any.at[:, pl.ds(0, width)], first_ref, sems.at[0])
+    last = pltpu.make_async_copy(sky_any.at[:, pl.ds(strip - width, width)], last_ref, sems.at[1])
+    first.start()
+    last.start()
+    number = owner_ref[...] * (8 * LANES) + local_ref[...]
+    asked_ref[...] = jnp.broadcast_to(number, asked_ref.shape)
+    first.wait()
+    last.wait()
 
 
 def plan_body(
@@ -145,9 +157,11 @@
 
 def sky_body(
     me_ref, asked_ref, low_ref, sky_ref, high_ref, pattern_ref, table_ref, turn_any, mix_any,
-    out_any, mid_ref, half_ref, left_ref, turn_ref, mix_ref, wide_ref, out_ref, asked_smem, sems,
+    out_any, mid_ref, half_ref, left_ref, turn_ref, mix_ref, wide_ref, out_ref, number_ref, asked_smem, sems,
 ):
-    ids = pltpu.make_async_copy(asked_ref, asked_smem, sems.at[0])
+    asked = asked_ref[...]
+    number_ref[...] = (lax.shift_right_logical(asked, 7) * (16 * LANES)) | (asked & (LANES - 1))
+    ids = pltpu.make_async_copy(number_ref, asked_smem, sems.at[0])
     turn = pltpu.make_async_copy(turn_any, turn_ref, sems.at[1])
     mix = pltpu.make_async_copy(mix_any.at[me_ref[0]], mix_ref, sems.at[2])
     for copy in (ids, turn, mix):
@@ -190,27 +204,26 @@
     ids.wait()
     turn.wait()
     group, vis = asked_ref.shape
-    steps = vis // 8
-
-    def step(n, carry):
-        dest, first = n // steps, n % steps * 8
-        both = []
-        for r in range(8):
-            tile = asked_smem[dest, first + r]
-            at = pl.multiple_of(tile // LANES * 16, 16)
-            v0 = tile % LANES
-            re, im = half_ref[pl.ds(at, 8), :], half_ref[pl.ds(at + 8, 8), :]
-            c, s = turn_ref[0, pl.ds(v0, 1), :], turn_ref[1, pl.ds(v0, 1), :]
-            both.append((re * c + im * s, im * c - re * s))
-        at = pl.ds(pl.multiple_of(n * 16, 16), 16)
-        for q in range(4):
-            for part in range(2):
-                lo = (2 * q + part) * LANES
-                pair = jnp.concatenate([both[q][part], both[q + 4][part]], axis=0)
-                left_ref[at, lo : lo + LANES] = pair.astype(BF16)
+
+    def step(dest, carry):
+        for n in range(vis // 8):
+            both = []
+            for r in range(8):
+                number = asked_smem[dest, 8 * n + r]
+                at = pl.multiple_of(lax.shift_right_logical(number, 7), 16)
+                v0 = number & (LANES - 1)
+                re, im = half_ref[pl.ds(at, 8), :], half_ref[pl.ds(at + 8, 8), :]
+                c, s = turn_ref[0, pl.ds(v0, 1), :], turn_ref[1, pl.ds(v0, 1), :]
+                both.append((re * c + im * s, im * c - re * s))
+            at = pl.ds(pl.multiple_of(dest * (2 * vis), 2 * vis) + 16 * n, 16)
+            for q in range(4):
+                for part in range(2):
+                    lo = (2 * q + part) * LANES
+                    pair = jnp.concatenate([both[q][part], both[q + 4][part]], axis=0)
+                    left_ref[at, lo : lo + LANES] = pair.astype(BF16)
         return carry
 
-    lax.fori_loop(0, group * steps, step, 0, unroll=4)
+    lax.fori_loop(0, group, step, 0)
     copies = []
     chunk = 256
     for i in range(group * vis * 2 // chunk):
@@ -316,7 +329,7 @@
 ANY = pl.ANY
 
 
-def call(body, name, outs, args, scratch=()):
+def call(body, outs, args, scratch=()):
     shapes = [
         pltpu.VMEM(s, d) if space is FAST else jax.ShapeDtypeStruct(s, d) for s, d, space in outs
     ]
@@ -327,7 +340,6 @@
         in_specs=[spec(space) for _, space in args],
         out_specs=[spec(space) for _, _, space in outs],
         scratch_shapes=list(scratch),
-        name=name,
     )(*[pltpu.with_memory_space_constraint(a, FAST) if space is FAST else a for a, space in args])
 
 
@@ -345,19 +357,27 @@
     sem = pltpu.SemaphoreType.DMA
     me = lax.axis_index(GROUP_AXES).astype(jnp.int32).reshape(1)
 
-    numbers = tile_owner[:, :, 0] * tiles_dev + tile_local
-    asked = exchange(jnp.broadcast_to(numbers, (group, vis)))
-
+    owners = tile_owner[:, :, 0]
+    asking, first, last = call(
+        ask_body,
+        [
+            ((group, vis), jnp.int32, None),
+            ((rows, HALO), BF16, FAST),
+            ((rows, HALO), BF16, FAST),
+        ],
+        [(owners, None), (tile_local, None), (sky_model, ANY)],
+        [sem((2,))],
+    )
+    asked = exchange(asking)
     count = lax.axis_size("beam")
     forward = [(i, i + 1) for i in range(count - 1)]
     backward = [(target, source) for source, target in forward]
-    low = lax.ppermute(sky_model[:, strip - HALO :], "beam", forward)
-    high = lax.ppermute(sky_model[:, :HALO], "beam", backward)
+    low = lax.ppermute(last, "beam", forward)
+    high = lax.ppermute(first, "beam", backward)
 
     table = first_table()
     put, live, sky_fast, pattern_fast, table_fast = call(
         plan_body,
-        "plan",
         [
             ((2 * group * cap, 2 * vis), BF16, FAST),
             ((2 * vis, cells), F32, FAST),
@@ -366,7 +386,7 @@
             (table.shape, BF16, FAST),
         ],
         [
-            (tile_owner[:, :, 0], None),
+            (owners, None),
             (vis_count, None),
             (sky_model, ANY),
             (beam_pattern[0], ANY),
@@ -377,7 +397,6 @@
     turn, mix = turn_table(), mix_table(group)
     (partial,) = call(
         sky_body,
-        "sky",
         [((group * 2 * vis, cells), BF16, ANY)],
         [
             (me, pltpu.SMEM),
@@ -398,6 +417,7 @@
             pltpu.VMEM(mix.shape[1:], BF16),
             pltpu.VMEM((8 * LANES, LANES), BF16),
             pltpu.VMEM((group * 2 * vis, cells), BF16),
+            pltpu.VMEM((group, vis), jnp.int32),
             pltpu.SMEM((group, vis), jnp.int32),
             sem((3 + group * 2 * vis // 256,)),
         ],
@@ -405,14 +425,12 @@
     tiles = exchange(partial.reshape(group, 2 * vis, cells))
     target, kernels_fast = call(
         target_body,
-        "target",
         [((1, 2 * group * cap), jnp.int32, FAST), ((vis * cells, cells), BF16, FAST)],
         [(me, pltpu.SMEM), (asked, FAST), (kernels.reshape(vis * cells, cells), ANY)],
         [sem],
     )
     residual, terms = call(
         visit_body,
-        "visit",
         [((2 * vis, cells), F32, None), ((2 * group * cap, cells), BF16, None)],
         [
             (tiles, FAST),
@@ -425,7 +443,6 @@
     arrived = exchange(terms.reshape(group, 2 * cap, cells))
     (dirty,) = call(
         dirty_body,
-        "dirty",
         [((2 * tiles_dev, cells), F32, ANY)],
         [(arrived.reshape(2 * group * cap, cells), FAST), (target, FAST)],
         [pltpu.VMEM((2 * tiles_dev, cells), F32), sem((8,))],

time: 109 us -> 99.4 us (0.912)
  Pallas kernels: 19.5 us -> 15.3 us
  starting transfers between devices: 54.8 us -> 51.5 us
  local copies, waits for them, and re-layouts: 1.6 us -> 0.01 us
    pallas_call x5 -> x6, Pallas kernels: 19.5 us -> 15.3 us  [call(): pl.pallas_call(body, out_shape=shapes, in_specs=[spec(space) for _, space...]
    all_to_all x2, starting transfers between devices: 46.3 us -> 43.6 us  [exchange(): lax.all_to_all(block, GROUP_AXES, split_axis=0, concat_axis=0, tiled=True)]
  transfers between devices with their start and end apart: 4 -> 4, of which waited for: 2 -> 2; matrix products, arithmetic and copies ran while one was open for 1% -> 0% of each run, Pallas kernels for 3% -> 4%
where the time goes in v3:
time: 99.4 us; the launch traced here: 98.9 us
  starting transfers between devices  51.5 us (52%)
  waiting for transfers between devices  20.5 us (21%)
  Pallas kernels  15.3 us (15%)
  blocking collectives  10.8 us (11%)
    all_to_all x2, starting transfers between devices, exchange(): lax.all_to_all(block, GROUP_AXES, split_axis=0, concat_axis=0, tiled=True)  43.6 us
    all_to_all x2, waiting for transfers between devices, exchange(): lax.all_to_all(block, GROUP_AXES, split_axis=0, concat_axis=0, tiled=True)  20.5 us
    pallas_call x6, Pallas kernels, call(): pl.pallas_call(body, out_shape=shapes, in_specs=[spec(space) for _, space...  15.3 us
    all_to_all x1, blocking collectives, exchange(): lax.all_to_all(block, GROUP_AXES, split_axis=0, concat_axis=0, tiled=True)  10.8 us
    ppermute x1, starting transfers between devices, on_device(): low = lax.ppermute(last, 'beam', forward)  6.57 us
  transfers between devices with their start and end apart: 4, of which 2 were waited for; matrix products, arithmetic and copies ran while one was open for 0% of the time, Pallas kernels for 4%

profile of v3, /device:TPU:65, one launch (start us, length us, event | category | flops | bytes accessed | tf_op | source)
XLA Modules:
  0.0 98.9 jit_solution(1952511587513327349)
XLA Ops:
  0.6 2.3 %shard_map.113 = (s32[16,64]{1,0:T(8,128)}, bf16[128,512]{1,0:T(8,128)(2,1)S(1)}, bf16[128,512]{1,0:T(8,128)(2,1)S(1)}) custom-call(s32[1,64]{1,0:T(1,128)} %bitcast.24, s32[1,64]{1,0:T(1,128)} %local_ref.1, bf16[128,1024]{1,0:T(8,128)(2,1)} %sky_any.3), custom_call_target="tpu_custom_call" | custom-call | tf_op jit(solution)/shard_map/pallas_call | solution.py:337
  2.9 6.6 %collective-permute-start = (bf16[128,512]{1,0:T(8,128)(2,1)S(1)}, bf16[128,512]{1,0:T(8,128)(2,1)S(1)}, u32[]{:S(2)}, u32[]{:S(2)}) collective-permute-start(bf16[128,512]{1,0:T(8,128)(2,1)S(1)} %get-tuple-element.15), channel_id=1, source_target_pairs={{0,16},{16,32},{32,48},{48,64},{64,80},{80,96},{96,112},{112,128},... | collective-permute-start | bytes 393224 | tf_op jit(solution)/shard_map/ppermute | solution.py:375
  9.5 1.3 %collective-permute-start.1 = (bf16[128,512]{1,0:T(8,128)(2,1)S(1)}, bf16[128,512]{1,0:T(8,128)(2,1)S(1)}, u32[]{:S(2)}, u32[]{:S(2)}) collective-permute-start(bf16[128,512]{1,0:T(8,128)(2,1)S(1)} %get-tuple-element.17), channel_id=1, source_target_pairs={{16,0},{32,16},{48,32},{64,48},{80,64},{96,80},{112,96},{128,112},... | collective-permute-start | bytes 393224 | tf_op jit(solution)/shard_map/ppermute | solution.py:376
  10.8 39.5 %all-to-all-start = ((s32[16,1,64]{2,1,0:T(1,128)}), s32[16,1,64]{2,1,0:T(1,128)S(1)}, u32[]{:S(2)}, u32[]{:S(2)}) async-start(s32[16,1,64]{2,1,0:T(1,128)} %bitcast.23), calls=%async_computation | async-start | bytes 16384 | tf_op jit(solution)/shard_map/all_to_all | solution.py:347
  50.2 2.2 %shard_map.114 = (bf16[256,128]{1,0:T(8,128)(2,1)S(1)}, f32[128,128]{1,0:T(8,128)S(1)}, bf16[128,1024]{1,0:T(8,128)(2,1)S(1)}, bf16[128,2048]{1,0:T(8,128)(2,1)S(1)}, bf16[8,256,256]{2,1,0:T(8,128)(2,1)S(1)}) custom-call(s32[1,64]{1,0:T(1,128)} %bitcast.25, s32[1,64]{1,0:T(1,128)} %count_ref.1, bf16[128,1024]{1,0:T(8,128)(2,1)} %sky_any.3, ...), custom_call_target="tpu_custom_call" | custom-call | tf_op jit(solution)/shard_map/pallas_call | solution.py:337
  52.4 4.9 %all-to-all-done = s32[16,1,64]{2,1,0:T(1,128)S(1)} async-done(((s32[16,1,64]{2,1,0:T(1,128)}), s32[16,1,64]{2,1,0:T(1,128)S(1)}, u32[]{:S(2)}, u32[]{:S(2)}) %all-to-all-start) | async-done | bytes 4128 | tf_op jit(solution)/shard_map/all_to_all | solution.py:347
  57.3 0.0 collective-permute-done.low_ref
  57.3 0.0 collective-permute-done.1.high_ref
  57.3 5.9 %shard_map.115 = bf16[2048,128]{1,0:T(8,128)(2,1)} custom-call(s32[1]{0:T(128)} %bitcast.me_ref, s32[16,64]{1,0:T(8,128)S(1)} %bitcast.15, bf16[128,512]{1,0:T(8,128)(2,1)S(1)} %collective-permute-done.low_ref, bf16[128,1024]{1,0:T(8,128)(2,1)S(1)} %get-tuple-element.16.sky_ref, bf16[128,512]{1,0:T(8,128)(2,1)S(1)} %collective-permute-done.1.high_ref, ...), custom_call_target="tpu_custom_call" | custom-call | tf_op jit(solution)/shard_map/pallas_call | solution.py:337
  63.3 0.0 copy-start
  63.3 4.2 %all-to-all-start.1 = ((bf16[16,128,128]{2,1,0:T(8,128)(2,1)}), bf16[16,128,128]{2,1,0:T(8,128)(2,1)S(1)}, u32[]{:S(2)}, u32[]{:S(2)}) async-start(bf16[16,128,128]{2,1,0:T(8,128)(2,1)} %bitcast.19), calls=%async_computation.1 | async-start | bytes 1048576 | tf_op jit(solution)/shard_map/all_to_all | solution.py:347
  67.5 1.6 %shard_map.116 = (s32[1,256]{1,0:T(1,128)S(1)}, bf16[8192,128]{1,0:T(8,128)(2,1)S(1)}) custom-call(s32[1]{0:T(128)} %bitcast.me_ref, s32[16,64]{1,0:T(8,128)S(1)} %bitcast.16, bf16[8192,128]{1,0:T(8,128)(2,1)} %bitcast.18), custom_call_target="tpu_custom_call" | custom-call | tf_op jit(solution)/shard_map/pallas_call | solution.py:337
  69.1 15.6 %all-to-all-done.1.tiles_ref = bf16[16,128,128]{2,1,0:T(8,128)(2,1)S(1)} async-done(((bf16[16,128,128]{2,1,0:T(8,128)(2,1)}), bf16[16,128,128]{2,1,0:T(8,128)(2,1)S(1)}, u32[]{:S(2)}, u32[]{:S(2)}) %all-to-all-start.1) | async-done | bytes 524320 | tf_op jit(solution)/shard_map/all_to_all | solution.py:347
  84.7 0.0 copy-done
  84.7 2.1 %shard_map.117 = (f32[128,128]{1,0:T(8,128)}, bf16[256,128]{1,0:T(8,128)(2,1)}) custom-call(bf16[16,128,128]{2,1,0:T(8,128)(2,1)S(1)} %all-to-all-done.1.tiles_ref, bf16[256,128]{1,0:T(8,128)(2,1)S(1)} %get-tuple-element.20.put_ref, f32[128,128]{1,0:T(8,128)S(1)} %get-tuple-element.21.live_ref, f32[128,128]{1,0:T(8,128)S(1)} %bitcast.17, ...), custom_call_target="tpu_custom_call" | custom-call | tf_op jit(solution)/shard_map/pallas_call | solution.py:337
  86.8 10.8 %all_to_all.21 = bf16[16,16,128]{2,1,0:T(8,128)(2,1)S(1)} all-to-all(bf16[16,16,128]{2,1,0:T(8,128)(2,1)} %bitcast.22), channel_id=1, replica_groups=mesh['tile'=2,'beam'=16,'bl'=8,'pol'=2] {'bl','pol'}, dimensions={0} | all-to-all | bytes 131072 | tf_op jit(solution)/shard_map/all_to_all | solution.py:347
  97.6 1.2 %shard_map.118 = f32[2048,128]{1,0:T(8,128)} custom-call(bf16[256,128]{1,0:T(8,128)(2,1)S(1)} %bitcast.14, s32[1,256]{1,0:T(1,128)S(1)} %get-tuple-element.25.target_ref), custom_call_target="tpu_custom_call" | custom-call | tf_op jit(solution)/shard_map/pallas_call | solution.py:337
Async XLA Ops:
  2.9 54.4 %collective-permute-start = (bf16[128,512]{1,0:T(8,128)(2,1)S(1)}, bf16[128,512]{1,0:T(8,128)(2,1)S(1)}, u32[]{:S(2)}, u32[]{:S(2)}) collective-permute-start(bf16[128,512]{1,0:T(8,128)(2,1)S(1)} %get-tuple-element.15), channel_id=1, source_target_pairs={{0,16},{16,32},{32,48},{48,64},{64,80},{80,96},{96,112},{112,128},... | collective-permute-start | bytes 393224 | tf_op jit(solution)/shard_map/ppermute | solution.py:375
  9.5 47.9 %collective-permute-start.1 = (bf16[128,512]{1,0:T(8,128)(2,1)S(1)}, bf16[128,512]{1,0:T(8,128)(2,1)S(1)}, u32[]{:S(2)}, u32[]{:S(2)}) collective-permute-start(bf16[128,512]{1,0:T(8,128)(2,1)S(1)} %get-tuple-element.17), channel_id=1, source_target_pairs={{16,0},{32,16},{48,32},{64,48},{80,64},{96,80},{112,96},{128,112},... | collective-permute-start | bytes 393224 | tf_op jit(solution)/shard_map/ppermute | solution.py:376
  10.8 46.5 %all-to-all-start = ((s32[16,1,64]{2,1,0:T(1,128)}), s32[16,1,64]{2,1,0:T(1,128)S(1)}, u32[]{:S(2)}, u32[]{:S(2)}) async-start(s32[16,1,64]{2,1,0:T(1,128)} %bitcast.23), calls=%async_computation | async-start | bytes 16384 | tf_op jit(solution)/shard_map/all_to_all | solution.py:347
  63.3 21.4 %copy-start = (f32[1,64,2,128]{3,2,1,0:T(2,128)S(1)}, f32[1,64,2,128]{3,2,1,0:T(2,128)}, u32[]{:S(2)}) copy-start(f32[1,64,2,128]{3,2,1,0:T(2,128)} %param.13) | copy-start | bytes 196612
  63.3 21.4 %all-to-all-start.1 = ((bf16[16,128,128]{2,1,0:T(8,128)(2,1)}), bf16[16,128,128]{2,1,0:T(8,128)(2,1)S(1)}, u32[]{:S(2)}, u32[]{:S(2)}) async-start(bf16[16,128,128]{2,1,0:T(8,128)(2,1)} %bitcast.19), calls=%async_computation.1 | async-start | bytes 1048576 | tf_op jit(solution)/shard_map/all_to_all | solution.py:347

commit v4 on v3

--- a/solution.py
+++ b/solution.py
@@ -1,3 +1,4 @@
+import functools
 import math
 
 import jax
@@ -110,26 +111,18 @@
     return lax.broadcasted_iota(jnp.int32, shape, dim)
 
 
-def ask_body(owner_ref, local_ref, sky_any, asked_ref, first_ref, last_ref, sems):
-    strip, width = sky_any.shape[1], first_ref.shape[1]
-    first = pltpu.make_async_copy(sky_any.at[:, pl.ds(0, width)], first_ref, sems.at[0])
-    last = pltpu.make_async_copy(sky_any.at[:, pl.ds(strip - width, width)], last_ref, sems.at[1])
-    first.start()
-    last.start()
+def ask_body(owner_ref, local_ref, asked_ref):
     number = owner_ref[...] * (8 * LANES) + local_ref[...]
     asked_ref[...] = jnp.broadcast_to(number, asked_ref.shape)
-    first.wait()
-    last.wait()
 
 
 def plan_body(
-    owner_ref, count_ref, sky_any, pattern_any, table_any,
-    put_ref, live_ref, sky_ref, pattern_ref, table_ref, sems,
+    owner_ref, count_ref, sky_any, pattern_any, put_ref, live_ref, sky_ref, pattern_ref, sems
 ):
     copies = [
         pltpu.make_async_copy(source, target, sems.at[i])
         for i, (source, target) in enumerate(
-            [(sky_any, sky_ref), (pattern_any, pattern_ref), (table_any, table_ref)]
+            [(sky_any, sky_ref), (pattern_any, pattern_ref)]
         )
     ]
     for copy in copies:
@@ -156,16 +149,10 @@
 
 
 def sky_body(
-    me_ref, asked_ref, low_ref, sky_ref, high_ref, pattern_ref, table_ref, turn_any, mix_any,
-    out_any, mid_ref, half_ref, left_ref, turn_ref, mix_ref, wide_ref, out_ref, number_ref, asked_smem, sems,
+    low_ref, sky_ref, high_ref, pattern_ref, table_any, out_ref, mid_ref, half_ref, table_ref, sem
 ):
-    asked = asked_ref[...]
-    number_ref[...] = (lax.shift_right_logical(asked, 7) * (16 * LANES)) | (asked & (LANES - 1))
-    ids = pltpu.make_async_copy(number_ref, asked_smem, sems.at[0])
-    turn = pltpu.make_async_copy(turn_any, turn_ref, sems.at[1])
-    mix = pltpu.make_async_copy(mix_any.at[me_ref[0]], mix_ref, sems.at[2])
-    for copy in (ids, turn, mix):
-        copy.start()
+    copy = pltpu.make_async_copy(table_any, table_ref, sem)
+    copy.start()
     rows = sky_ref.shape[0]
     block = 16
     for start in range(0, rows, block):
@@ -188,47 +175,75 @@
             mid_ref[p, at, :LANES] = out[p][0].astype(BF16)
             mid_ref[p, at, LANES:] = out[p][1].astype(BF16)
     per = GRID // 2 // RADIX
+    copy.wait()
     for p in range(RADIX // 2):
-        half = dot(table_ref[p], mid_ref[p], ((1,), (1,))).astype(BF16).astype(F32)
+        half = dot(table_ref[p], mid_ref[p], ((1,), (1,)))
         for c in range(2):
             for s in range(2):
                 i = p if s == 0 else (8 - p) % 8
                 first = (2 * c + s) * per
                 half_ref[pl.ds(16 * s + 8 * c + i, per, stride=32), :] = half[first : first + per]
-    mix.wait()
+    out_ref[...] = half_ref[...].astype(BF16)
+
+
+def share_body(
+    me_ref, asked_ref, half_ref, turn_any, mix_any, *rest, partner
+):
+    if partner:
+        sum_ref, out_any = rest[:2]
+        rest = rest[2:]
+    else:
+        out_any = rest[0]
+        rest = rest[1:]
+    left_ref, turn_ref, mix_ref, wide_ref, out_ref, number_ref, asked_smem, sems = rest
+    me = me_ref[0]
+    asked = asked_ref[...]
+    number_ref[...] = (lax.shift_right_logical(asked, 7) * (16 * LANES)) | (asked & (LANES - 1))
+    ids = pltpu.make_async_copy(number_ref, asked_smem, sems.at[0])
+    turn = pltpu.make_async_copy(turn_any, turn_ref, sems.at[1])
+    source = me ^ 1 if partner else me
+    mix = pltpu.make_async_copy(mix_any.at[source], mix_ref, sems.at[2])
+    for copy in (ids, turn, mix):
+        copy.start()
+    for copy in (ids, turn, mix):
+        copy.wait()
     quarter = LANES // 4
     for q in range(4):
         held = mix_ref[...].astype(F32)
         lane = iota(held.shape, 1) // quarter == q
         wide_ref[2 * LANES * q : 2 * LANES * (q + 1), :] = jnp.where(lane, held, 0.0).astype(BF16)
-    ids.wait()
-    turn.wait()
     group, vis = asked_ref.shape
-
-    def step(dest, carry):
+    parity = me & 1
+
+    def step(pair, carry):
+        dest = 2 * pair + parity
         for n in range(vis // 8):
             both = []
             for r in range(8):
                 number = asked_smem[dest, 8 * n + r]
                 at = pl.multiple_of(lax.shift_right_logical(number, 7), 16)
                 v0 = number & (LANES - 1)
-                re, im = half_ref[pl.ds(at, 8), :], half_ref[pl.ds(at + 8, 8), :]
+                cells = half_ref[pl.ds(at, 16), :].astype(F32)
+                re, im = cells[:8], cells[8:]
                 c, s = turn_ref[0, pl.ds(v0, 1), :], turn_ref[1, pl.ds(v0, 1), :]
                 both.append((re * c + im * s, im * c - re * s))
-            at = pl.ds(pl.multiple_of(dest * (2 * vis), 2 * vis) + 16 * n, 16)
+            at = pl.ds(pl.multiple_of(pair * (2 * vis), 2 * vis) + 16 * n, 16)
             for q in range(4):
                 for part in range(2):
                     lo = (2 * q + part) * LANES
-                    pair = jnp.concatenate([both[q][part], both[q + 4][part]], axis=0)
-                    left_ref[at, lo : lo + LANES] = pair.astype(BF16)
+                    two = jnp.concatenate([both[q][part], both[q + 4][part]], axis=0)
+                    left_ref[at, lo : lo + LANES] = two.astype(BF16)
         return carry
 
-    lax.fori_loop(0, group, step, 0)
+    lax.fori_loop(0, group // 2, step, 0)
+    if not partner:
+        out_any[...] = dot(left_ref[...], wide_ref[...])
+        return
     copies = []
     chunk = 256
-    for i in range(group * vis * 2 // chunk):
+    for i in range(group * vis // chunk):
         at = pl.ds(i * chunk, chunk)
-        out_ref[at, :] = dot(left_ref[at, :], wide_ref[...]).astype(BF16)
+        out_ref[at, :] = (sum_ref[at, :] + dot(left_ref[at, :], wide_ref[...])).astype(BF16)
         copies.append(pltpu.make_async_copy(out_ref.at[at], out_any.at[at], sems.at[3 + i]))
         copies[-1].start()
     for copy in copies:
@@ -343,8 +358,8 @@
     )(*[pltpu.with_memory_space_constraint(a, FAST) if space is FAST else a for a, space in args])
 
 
-def exchange(block):
-    return lax.all_to_all(block, GROUP_AXES, split_axis=0, concat_axis=0, tiled=True)
+def exchange(block, axes=GROUP_AXES):
+    return lax.all_to_all(block, axes, split_axis=0, concat_axis=0, tiled=True)
 
 
 def on_device(sky_model, beam_pattern, kernels, observed, tile_owner, tile_local, vis_count):
@@ -358,71 +373,70 @@
     me = lax.axis_index(GROUP_AXES).astype(jnp.int32).reshape(1)
 
     owners = tile_owner[:, :, 0]
-    asking, first, last = call(
-        ask_body,
-        [
-            ((group, vis), jnp.int32, None),
-            ((rows, HALO), BF16, FAST),
-            ((rows, HALO), BF16, FAST),
-        ],
-        [(owners, None), (tile_local, None), (sky_model, ANY)],
-        [sem((2,))],
-    )
-    asked = exchange(asking)
+    (asking,) = call(
+        ask_body, [((group, vis), jnp.int32, None)], [(owners, None), (tile_local, None)]
+    )
     count = lax.axis_size("beam")
     forward = [(i, i + 1) for i in range(count - 1)]
     backward = [(target, source) for source, target in forward]
-    low = lax.ppermute(last, "beam", forward)
-    high = lax.ppermute(first, "beam", backward)
+    low = lax.ppermute(sky_model[:, strip - HALO :], "beam", forward)
+    high = lax.ppermute(sky_model[:, :HALO], "beam", backward)
+    asked = exchange(asking)
 
     table = first_table()
-    put, live, sky_fast, pattern_fast, table_fast = call(
+    put, live, sky_fast, pattern_fast = call(
         plan_body,
         [
             ((2 * group * cap, 2 * vis), BF16, FAST),
             ((2 * vis, cells), F32, FAST),
             ((rows, strip), BF16, FAST),
             ((rows, GRID), BF16, FAST),
-            (table.shape, BF16, FAST),
         ],
         [
             (owners, None),
             (vis_count, None),
             (sky_model, ANY),
             (beam_pattern[0], ANY),
-            (table, ANY),
         ],
-        [sem((3,))],
-    )
-    turn, mix = turn_table(), mix_table(group)
-    (partial,) = call(
+        [sem((2,))],
+    )
+    (half,) = call(
         sky_body,
-        [((group * 2 * vis, cells), BF16, ANY)],
-        [
-            (me, pltpu.SMEM),
-            (asked, FAST),
-            (low, FAST),
-            (sky_fast, FAST),
-            (high, FAST),
-            (pattern_fast, FAST),
-            (table_fast, FAST),
-            (turn, ANY),
-            (mix, ANY),
-        ],
+        [((GRID, LANES), BF16, FAST)],
+        [(low, FAST), (sky_fast, FAST), (high, FAST), (pattern_fast, FAST), (table, ANY)],
         [
             pltpu.VMEM((RADIX // 2, rows, 2 * LANES), BF16),
             pltpu.VMEM((GRID, LANES), F32),
-            pltpu.VMEM((group * 2 * vis, 8 * LANES), BF16),
-            pltpu.VMEM(turn.shape, F32),
-            pltpu.VMEM(mix.shape[1:], BF16),
-            pltpu.VMEM((8 * LANES, LANES), BF16),
-            pltpu.VMEM((group * 2 * vis, cells), BF16),
-            pltpu.VMEM((group, vis), jnp.int32),
-            pltpu.SMEM((group, vis), jnp.int32),
-            sem((3 + group * 2 * vis // 256,)),
+            pltpu.VMEM(table.shape, BF16),
+            sem,
         ],
     )
-    tiles = exchange(partial.reshape(group, 2 * vis, cells))
+    other = lax.ppermute(half, "pol", [(0, 1), (1, 0)])
+    turn, mix = turn_table(), mix_table(group)
+    served = group * vis
+    scratch = [
+        pltpu.VMEM((served, 8 * LANES), BF16),
+        pltpu.VMEM(turn.shape, F32),
+        pltpu.VMEM(mix.shape[1:], BF16),
+        pltpu.VMEM((8 * LANES, LANES), BF16),
+        pltpu.VMEM((served, cells), BF16),
+        pltpu.VMEM((group, vis), jnp.int32),
+        pltpu.SMEM((group, vis), jnp.int32),
+        sem((3 + served // 256,)),
+    ]
+    (own_sum,) = call(
+        functools.partial(share_body, partner=False),
+        [((served, cells), F32, FAST)],
+        [(me, pltpu.SMEM), (asked, FAST), (half, FAST), (turn, ANY), (mix, ANY)],
+        scratch,
+    )
+    (partial,) = call(
+        functools.partial(share_body, partner=True),
+        [((served, cells), BF16, ANY)],
+        [(me, pltpu.SMEM), (asked, FAST), (other, FAST), (turn, ANY), (mix, ANY), (own_sum, FAST)],
+        scratch,
+    )
+    tiles = exchange(partial.reshape(group // 2, 2 * vis, cells), "bl")
     target, kernels_fast = call(
         target_body,
         [((1, 2 * group * cap), jnp.int32, FAST), ((vis * cells, cells), BF16, FAST)],

time: 99.4 us -> 105 us (1.056)
  starting transfers between devices: 51.5 us -> 57.1 us
  waiting for transfers between devices: 20.5 us -> 16 us
  blocking collectives: 10.8 us -> 13 us
  Pallas kernels: 15.3 us -> 16.8 us
    ppermute x2 -> x3, starting transfers between devices: 7.88 us -> 49.8 us  [the longest x1 41.3 us: on_device(): other = lax.ppermute(half, 'pol', [(0, 1), (1, 0)])]
    all_to_all x2, starting transfers between devices: 43.6 us -> 7.26 us  [exchange(): return lax.all_to_all(block, axes, split_axis=0, concat_axis=0, tiled=True)]
    all_to_all x2, waiting for transfers between devices: 20.5 us -> 15.9 us  [exchange(): return lax.all_to_all(block, axes, split_axis=0, concat_axis=0, tiled=True)]
    all_to_all x1, blocking collectives: 10.8 us -> 13 us  [exchange(): return lax.all_to_all(block, axes, split_axis=0, concat_axis=0, tiled=True)]
    pallas_call x6 -> x8, Pallas kernels: 15.3 us -> 16.8 us  [call(): pl.pallas_call(body, out_shape=shapes, in_specs=[spec(space) for _, space...]
  transfers between devices with their start and end apart: 4 -> 5, of which waited for: 2 -> 3; matrix products, arithmetic and copies ran while one was open for 0% -> 0% of each run, Pallas kernels for 4% -> 7%
where the time goes in v4:
time: 105 us
  starting transfers between devices  57.1 us (54%)
  Pallas kernels  16.8 us (16%)
  waiting for transfers between devices  16 us (15%)
  blocking collectives  13 us (12%)
    ppermute x1, starting transfers between devices, on_device(): other = lax.ppermute(half, 'pol', [(0, 1), (1, 0)])  41.3 us
    pallas_call x8, Pallas kernels, call(): pl.pallas_call(body, out_shape=shapes, in_specs=[spec(space) for _, space...  16.8 us
    all_to_all x2, waiting for transfers between devices, exchange(): return lax.all_to_all(block, axes, split_axis=0, concat_axis=0, tiled=True)  15.9 us
    all_to_all x1, blocking collectives, exchange(): return lax.all_to_all(block, axes, split_axis=0, concat_axis=0, tiled=True)  13 us
    all_to_all x2, starting transfers between devices, exchange(): return lax.all_to_all(block, axes, split_axis=0, concat_axis=0, tiled=True)  7.26 us
    ppermute x1, starting transfers between devices, on_device(): low = lax.ppermute(sky_model[:, strip - HALO:], 'beam', forward)  7.21 us
  transfers between devices with their start and end apart: 5, of which 3 were waited for; matrix products, arithmetic and copies ran while one was open for 0% of the time, Pallas kernels for 7%

profile of v4, /device:TPU:65, one launch (start us, length us, event | category | flops | bytes accessed | tf_op | source)
XLA Modules:
  0.0 104.6 jit_solution(13625890711839311691)
XLA Ops:
  0.6 1.0 fusion
  1.6 1.3 %collective-permute-start.1 = (bf16[128,512]{1,0:T(8,128)(2,1)S(1)}, bf16[128,512]{1,0:T(8,128)(2,1)S(1)}, u32[]{:S(2)}, u32[]{:S(2)}) collective-permute-start(bf16[128,512]{1,0:T(8,128)(2,1)S(1)} %get-tuple-element.18), channel_id=1, source_target_pairs={{16,0},{32,16},{48,32},{64,48},{80,64},{96,80},{112,96},{128,112},... | collective-permute-start | bytes 393224 | tf_op jit(solution)/shard_map/ppermute | solution.py:383
  2.9 7.2 %collective-permute-start = (bf16[128,512]{1,0:T(8,128)(2,1)S(1)}, bf16[128,512]{1,0:T(8,128)(2,1)S(1)}, u32[]{:S(2)}, u32[]{:S(2)}) collective-permute-start(bf16[128,512]{1,0:T(8,128)(2,1)S(1)} %get-tuple-element.19), channel_id=1, source_target_pairs={{0,16},{16,32},{32,48},{48,64},{64,80},{80,96},{96,112},{112,128},... | collective-permute-start | bytes 393224 | tf_op jit(solution)/shard_map/ppermute | solution.py:382
  10.2 1.8 %shard_map.114 = (bf16[256,128]{1,0:T(8,128)(2,1)S(1)}, f32[128,128]{1,0:T(8,128)S(1)}, bf16[128,1024]{1,0:T(8,128)(2,1)S(1)}, bf16[128,2048]{1,0:T(8,128)(2,1)S(1)}) custom-call(s32[1,64]{1,0:T(1,128)} %bitcast.25, s32[1,64]{1,0:T(1,128)} %count_ref.1, bf16[128,1024]{1,0:T(8,128)(2,1)} %sky_any.1, bf16[128,2048]{1,0:T(8,128)(2,1)} %bitcast.22), custom_call_target="tpu_custom_call" | custom-call | tf_op jit(solution)/shard_map/pallas_call | solution.py:352
  12.0 0.0 collective-permute-done.1.high_ref
  12.0 0.1 collective-permute-done.low_ref
  12.1 2.2 %shard_map.115.half_ref = bf16[2048,128]{1,0:T(8,128)(2,1)S(1)} custom-call(bf16[128,512]{1,0:T(8,128)(2,1)S(1)} %collective-permute-done.low_ref, bf16[128,1024]{1,0:T(8,128)(2,1)S(1)} %get-tuple-element.10.sky_ref, bf16[128,512]{1,0:T(8,128)(2,1)S(1)} %collective-permute-done.1.high_ref, bf16[128,2048]{1,0:T(8,128)(2,1)S(1)} %get-tuple-element.11.pattern_ref, ...), custom_call_target="tpu_custom_call" | custom-call | tf_op jit(solution)/shard_map/pallas_call | solution.py:352
  14.4 41.3 %collective-permute-start.2 = (bf16[2048,128]{1,0:T(8,128)(2,1)S(1)}, bf16[2048,128]{1,0:T(8,128)(2,1)S(1)}, u32[]{:S(2)}, u32[]{:S(2)}) collective-permute-start(bf16[2048,128]{1,0:T(8,128)(2,1)S(1)} %shard_map.115.half_ref), channel_id=1, source_target_pairs={{0,1},{1,0},{2,3},{3,2},{4,5},{5,4},{6,7},{7,6},{8,9},{9,8},{10,11... | collective-permute-start | bytes 1572872 | tf_op jit(solution)/shard_map/ppermute | solution.py:414
  55.6 1.3 %shard_map.113 = s32[16,64]{1,0:T(8,128)} custom-call(s32[1,64]{1,0:T(1,128)} %bitcast.26, s32[1,64]{1,0:T(1,128)} %local_ref.1), custom_call_target="tpu_custom_call" | custom-call | tf_op jit(solution)/shard_map/pallas_call | solution.py:352
  56.9 3.6 %all-to-all-start = ((s32[16,1,64]{2,1,0:T(1,128)}), s32[16,1,64]{2,1,0:T(1,128)S(1)}, u32[]{:S(2)}, u32[]{:S(2)}) async-start(s32[16,1,64]{2,1,0:T(1,128)} %bitcast.24), calls=%async_computation | async-start | bytes 16384 | tf_op jit(solution)/shard_map/all_to_all | solution.py:362
  60.6 6.7 %all-to-all-done = s32[16,1,64]{2,1,0:T(1,128)S(1)} async-done(((s32[16,1,64]{2,1,0:T(1,128)}), s32[16,1,64]{2,1,0:T(1,128)S(1)}, u32[]{:S(2)}, u32[]{:S(2)}) %all-to-all-start) | async-done | bytes 4128 | tf_op jit(solution)/shard_map/all_to_all | solution.py:362
  67.3 2.9 %shard_map.116.rest_0_ = f32[1024,128]{1,0:T(8,128)S(1)} custom-call(s32[1]{0:T(128)} %bitcast.me_ref, s32[16,64]{1,0:T(8,128)S(1)} %bitcast.15, bf16[2048,128]{1,0:T(8,128)(2,1)S(1)} %shard_map.115.half_ref, f32[2,128,128]{2,1,0:T(8,128)} %constant.17.clone.turn_any, bf16[16,256,128]{2,1,0:T(8,128)(2,1)} %constant.18.clone.mix_any), custom_call_target="tpu_custom_call" | custom-call | tf_op jit(solution)/shard_map/pallas_call | solution.py:352
  70.2 0.0 copy-start
  70.2 0.0 collective-permute-done.2.half_ref
  70.2 3.6 %shard_map.117 = bf16[1024,128]{1,0:T(8,128)(2,1)} custom-call(s32[1]{0:T(128)} %bitcast.me_ref, s32[16,64]{1,0:T(8,128)S(1)} %bitcast.16, bf16[2048,128]{1,0:T(8,128)(2,1)S(1)} %collective-permute-done.2.half_ref, f32[2,128,128]{2,1,0:T(8,128)} %constant.17.clone.turn_any, bf16[16,256,128]{2,1,0:T(8,128)(2,1)} %constant.18.clone.mix_any, ...), custom_call_target="tpu_custom_call" | custom-call | tf_op jit(solution)/shard_map/pallas_call | solution.py:352
  73.9 3.6 %all-to-all-start.1 = ((bf16[8,128,128]{2,1,0:T(8,128)(2,1)}), bf16[8,128,128]{2,1,0:T(8,128)(2,1)S(1)}, u32[]{:S(2)}, u32[]{:S(2)}) async-start(bf16[8,128,128]{2,1,0:T(8,128)(2,1)} %bitcast.21), calls=%async_computation.1 | async-start | bytes 524288 | tf_op jit(solution)/shard_map/all_to_all | solution.py:362
  77.5 1.6 %shard_map.118 = (s32[1,256]{1,0:T(1,128)S(1)}, bf16[8192,128]{1,0:T(8,128)(2,1)S(1)}) custom-call(s32[1]{0:T(128)} %bitcast.me_ref, s32[16,64]{1,0:T(8,128)S(1)} %bitcast.17, bf16[8192,128]{1,0:T(8,128)(2,1)} %bitcast.19), custom_call_target="tpu_custom_call" | custom-call | tf_op jit(solution)/shard_map/pallas_call | solution.py:352
  79.1 9.2 %all-to-all-done.1.tiles_ref = bf16[8,128,128]{2,1,0:T(8,128)(2,1)S(1)} async-done(((bf16[8,128,128]{2,1,0:T(8,128)(2,1)}), bf16[8,128,128]{2,1,0:T(8,128)(2,1)S(1)}, u32[]{:S(2)}, u32[]{:S(2)}) %all-to-all-start.1) | async-done | bytes 262176 | tf_op jit(solution)/shard_map/all_to_all | solution.py:362
  88.3 0.0 copy-done
  88.3 2.1 %shard_map.119 = (f32[128,128]{1,0:T(8,128)}, bf16[256,128]{1,0:T(8,128)(2,1)}) custom-call(bf16[8,128,128]{2,1,0:T(8,128)(2,1)S(1)} %all-to-all-done.1.tiles_ref, bf16[256,128]{1,0:T(8,128)(2,1)S(1)} %get-tuple-element.12.put_ref, f32[128,128]{1,0:T(8,128)S(1)} %get-tuple-element.13.live_ref, f32[128,128]{1,0:T(8,128)S(1)} %bitcast.18, ...), custom_call_target="tpu_custom_call" | custom-call | tf_op jit(solution)/shard_map/pallas_call | solution.py:352
  90.4 13.0 %all_to_all.21 = bf16[16,16,128]{2,1,0:T(8,128)(2,1)S(1)} all-to-all(bf16[16,16,128]{2,1,0:T(8,128)(2,1)} %bitcast.23), channel_id=1, replica_groups=mesh['tile'=2,'beam'=16,'bl'=8,'pol'=2] {'bl','pol'}, dimensions={0} | all-to-all | bytes 131072 | tf_op jit(solution)/shard_map/all_to_all | solution.py:362
  103.4 1.2 %shard_map.120 = f32[2048,128]{1,0:T(8,128)} custom-call(bf16[256,128]{1,0:T(8,128)(2,1)S(1)} %bitcast.14, s32[1,256]{1,0:T(1,128)S(1)} %get-tuple-element.17.target_ref), custom_call_target="tpu_custom_call" | custom-call | tf_op jit(solution)/shard_map/pallas_call | solution.py:352
Async XLA Ops:
  1.6 10.4 %collective-permute-start.1 = (bf16[128,512]{1,0:T(8,128)(2,1)S(1)}, bf16[128,512]{1,0:T(8,128)(2,1)S(1)}, u32[]{:S(2)}, u32[]{:S(2)}) collective-permute-start(bf16[128,512]{1,0:T(8,128)(2,1)S(1)} %get-tuple-element.18), channel_id=1, source_target_pairs={{16,0},{32,16},{48,32},{64,48},{80,64},{96,80},{112,96},{128,112},... | collective-permute-start | bytes 393224 | tf_op jit(solution)/shard_map/ppermute | solution.py:383
  2.9 9.2 %collective-permute-start = (bf16[128,512]{1,0:T(8,128)(2,1)S(1)}, bf16[128,512]{1,0:T(8,128)(2,1)S(1)}, u32[]{:S(2)}, u32[]{:S(2)}) collective-permute-start(bf16[128,512]{1,0:T(8,128)(2,1)S(1)} %get-tuple-element.19), channel_id=1, source_target_pairs={{0,16},{16,32},{32,48},{48,64},{64,80},{80,96},{96,112},{112,128},... | collective-permute-start | bytes 393224 | tf_op jit(solution)/shard_map/ppermute | solution.py:382
  14.4 55.9 %collective-permute-start.2 = (bf16[2048,128]{1,0:T(8,128)(2,1)S(1)}, bf16[2048,128]{1,0:T(8,128)(2,1)S(1)}, u32[]{:S(2)}, u32[]{:S(2)}) collective-permute-start(bf16[2048,128]{1,0:T(8,128)(2,1)S(1)} %shard_map.115.half_ref), channel_id=1, source_target_pairs={{0,1},{1,0},{2,3},{3,2},{4,5},{5,4},{6,7},{7,6},{8,9},{9,8},{10,11... | collective-permute-start | bytes 1572872 | tf_op jit(solution)/shard_map/ppermute | solution.py:414
  56.9 10.4 %all-to-all-start = ((s32[16,1,64]{2,1,0:T(1,128)}), s32[16,1,64]{2,1,0:T(1,128)S(1)}, u32[]{:S(2)}, u32[]{:S(2)}) async-start(s32[16,1,64]{2,1,0:T(1,128)} %bitcast.24), calls=%async_computation | async-start | bytes 16384 | tf_op jit(solution)/shard_map/all_to_all | solution.py:362
  70.2 18.1 %copy-start = (f32[1,64,2,128]{3,2,1,0:T(2,128)S(1)}, f32[1,64,2,128]{3,2,1,0:T(2,128)}, u32[]{:S(2)}) copy-start(f32[1,64,2,128]{3,2,1,0:T(2,128)} %param.13) | copy-start | bytes 196612
  73.9 14.4 %all-to-all-start.1 = ((bf16[8,128,128]{2,1,0:T(8,128)(2,1)}), bf16[8,128,128]{2,1,0:T(8,128)(2,1)S(1)}, u32[]{:S(2)}, u32[]{:S(2)}) async-start(bf16[8,128,128]{2,1,0:T(8,128)(2,1)} %bitcast.21), calls=%async_computation.1 | async-start | bytes 524288 | tf_op jit(solution)/shard_map/all_to_all | solution.py:362

commit v5 on v4

--- a/solution.py
+++ b/solution.py
@@ -1,4 +1,3 @@
-import functools
 import math
 
 import jax
@@ -111,22 +110,26 @@
     return lax.broadcasted_iota(jnp.int32, shape, dim)
 
 
-def ask_body(owner_ref, local_ref, asked_ref):
+def front_body(
+    me_ref, owner_ref, local_ref, count_ref, sky_any, pattern_any, turn_any, mix_any,
+    asked_ref, first_ref, last_ref, put_ref, live_ref, sky_ref, pattern_ref, turn_ref, mix_ref, sems,
+):
+    me = me_ref[0]
+    strip, width = sky_any.shape[1], first_ref.shape[1]
+    pairs = [
+        (sky_any.at[:, pl.ds(0, width)], first_ref),
+        (sky_any.at[:, pl.ds(strip - width, width)], last_ref),
+        (sky_any, sky_ref),
+        (pattern_any, pattern_ref),
+        (turn_any, turn_ref),
+        (mix_any.at[me], mix_ref.at[0]),
+        (mix_any.at[me ^ 1], mix_ref.at[1]),
+    ]
+    copies = [pltpu.make_async_copy(a, b, sems.at[i]) for i, (a, b) in enumerate(pairs)]
+    for copy in copies:
+        copy.start()
     number = owner_ref[...] * (8 * LANES) + local_ref[...]
     asked_ref[...] = jnp.broadcast_to(number, asked_ref.shape)
-
-
-def plan_body(
-    owner_ref, count_ref, sky_any, pattern_any, put_ref, live_ref, sky_ref, pattern_ref, sems
-):
-    copies = [
-        pltpu.make_async_copy(source, target, sems.at[i])
-        for i, (source, target) in enumerate(
-            [(sky_any, sky_ref), (pattern_any, pattern_ref)]
-        )
-    ]
-    for copy in copies:
-        copy.start()
     n = owner_ref.shape[1]
     wide, rows = put_ref.shape
     cap = wide // (2 * GRID // LANES)
@@ -187,33 +190,24 @@
 
 
 def share_body(
-    me_ref, asked_ref, half_ref, turn_any, mix_any, *rest, partner
+    me_ref, asked_ref, own_ref, other_ref, turn_ref, mix_ref, out_any,
+    left_ref, wide_ref, out_ref, number_ref, asked_smem, sems,
 ):
-    if partner:
-        sum_ref, out_any = rest[:2]
-        rest = rest[2:]
-    else:
-        out_any = rest[0]
-        rest = rest[1:]
-    left_ref, turn_ref, mix_ref, wide_ref, out_ref, number_ref, asked_smem, sems = rest
-    me = me_ref[0]
     asked = asked_ref[...]
     number_ref[...] = (lax.shift_right_logical(asked, 7) * (16 * LANES)) | (asked & (LANES - 1))
     ids = pltpu.make_async_copy(number_ref, asked_smem, sems.at[0])
-    turn = pltpu.make_async_copy(turn_any, turn_ref, sems.at[1])
-    source = me ^ 1 if partner else me
-    mix = pltpu.make_async_copy(mix_any.at[source], mix_ref, sems.at[2])
-    for copy in (ids, turn, mix):
-        copy.start()
-    for copy in (ids, turn, mix):
-        copy.wait()
+    ids.start()
+    halves = (own_ref, other_ref)
     quarter = LANES // 4
-    for q in range(4):
-        held = mix_ref[...].astype(F32)
-        lane = iota(held.shape, 1) // quarter == q
-        wide_ref[2 * LANES * q : 2 * LANES * (q + 1), :] = jnp.where(lane, held, 0.0).astype(BF16)
+    for core in range(2):
+        held = mix_ref[core].astype(F32)
+        for q in range(4):
+            lane = iota(held.shape, 1) // quarter == q
+            at = pl.ds(2 * LANES * (4 * core + q), 2 * LANES)
+            wide_ref[at, :] = jnp.where(lane, held, 0.0).astype(BF16)
+    ids.wait()
     group, vis = asked_ref.shape
-    parity = me & 1
+    parity = me_ref[0] & 1
 
     def step(pair, carry):
         dest = 2 * pair + parity
@@ -223,28 +217,29 @@
                 number = asked_smem[dest, 8 * n + r]
                 at = pl.multiple_of(lax.shift_right_logical(number, 7), 16)
                 v0 = number & (LANES - 1)
-                cells = half_ref[pl.ds(at, 16), :].astype(F32)
-                re, im = cells[:8], cells[8:]
                 c, s = turn_ref[0, pl.ds(v0, 1), :], turn_ref[1, pl.ds(v0, 1), :]
-                both.append((re * c + im * s, im * c - re * s))
+                turned = []
+                for half_ref in halves:
+                    cells = half_ref[pl.ds(at, 16), :].astype(F32)
+                    re, im = cells[:8], cells[8:]
+                    turned += [re * c + im * s, im * c - re * s]
+                both.append(turned)
             at = pl.ds(pl.multiple_of(pair * (2 * vis), 2 * vis) + 16 * n, 16)
-            for q in range(4):
-                for part in range(2):
-                    lo = (2 * q + part) * LANES
-                    two = jnp.concatenate([both[q][part], both[q + 4][part]], axis=0)
-                    left_ref[at, lo : lo + LANES] = two.astype(BF16)
+            for core in range(2):
+                for q in range(4):
+                    for part in range(2):
+                        lo = (8 * core + 2 * q + part) * LANES
+                        two = [both[q][2 * core + part], both[q + 4][2 * core + part]]
+                        left_ref[at, lo : lo + LANES] = jnp.concatenate(two, axis=0).astype(BF16)
         return carry
 
     lax.fori_loop(0, group // 2, step, 0)
-    if not partner:
-        out_any[...] = dot(left_ref[...], wide_ref[...])
-        return
     copies = []
     chunk = 256
     for i in range(group * vis // chunk):
         at = pl.ds(i * chunk, chunk)
-        out_ref[at, :] = (sum_ref[at, :] + dot(left_ref[at, :], wide_ref[...])).astype(BF16)
-        copies.append(pltpu.make_async_copy(out_ref.at[at], out_any.at[at], sems.at[3 + i]))
+        out_ref[at, :] = dot(left_ref[at, :], wide_ref[...]).astype(BF16)
+        copies.append(pltpu.make_async_copy(out_ref.at[at], out_any.at[at], sems.at[1 + i]))
         copies[-1].start()
     for copy in copies:
         copy.wait()
@@ -372,34 +367,40 @@
     sem = pltpu.SemaphoreType.DMA
     me = lax.axis_index(GROUP_AXES).astype(jnp.int32).reshape(1)
 
-    owners = tile_owner[:, :, 0]
-    (asking,) = call(
-        ask_body, [((group, vis), jnp.int32, None)], [(owners, None), (tile_local, None)]
-    )
-    count = lax.axis_size("beam")
-    forward = [(i, i + 1) for i in range(count - 1)]
-    backward = [(target, source) for source, target in forward]
-    low = lax.ppermute(sky_model[:, strip - HALO :], "beam", forward)
-    high = lax.ppermute(sky_model[:, :HALO], "beam", backward)
-    asked = exchange(asking)
-
-    table = first_table()
-    put, live, sky_fast, pattern_fast = call(
-        plan_body,
-        [
+    turn, mix = turn_table(), mix_table(group)
+    asking, first, last, put, live, sky_fast, pattern_fast, turn_fast, mix_fast = call(
+        front_body,
+        [
+            ((group, vis), jnp.int32, None),
+            ((rows, HALO), BF16, FAST),
+            ((rows, HALO), BF16, FAST),
             ((2 * group * cap, 2 * vis), BF16, FAST),
             ((2 * vis, cells), F32, FAST),
             ((rows, strip), BF16, FAST),
             ((rows, GRID), BF16, FAST),
-        ],
-        [
-            (owners, None),
+            (turn.shape, F32, FAST),
+            ((2,) + mix.shape[1:], BF16, FAST),
+        ],
+        [
+            (me, pltpu.SMEM),
+            (tile_owner[:, :, 0], None),
+            (tile_local, None),
             (vis_count, None),
             (sky_model, ANY),
             (beam_pattern[0], ANY),
-        ],
-        [sem((2,))],
-    )
+            (turn, ANY),
+            (mix, ANY),
+        ],
+        [sem((7,))],
+    )
+    count = lax.axis_size("beam")
+    forward = [(i, i + 1) for i in range(count - 1)]
+    backward = [(target, source) for source, target in forward]
+    low = lax.ppermute(last, "beam", forward)
+    high = lax.ppermute(first, "beam", backward)
+    asked = exchange(asking)
+
+    table = first_table()
     (half,) = call(
         sky_body,
         [((GRID, LANES), BF16, FAST)],
@@ -412,29 +413,26 @@
         ],
     )
     other = lax.ppermute(half, "pol", [(0, 1), (1, 0)])
-    turn, mix = turn_table(), mix_table(group)
     served = group * vis
-    scratch = [
-        pltpu.VMEM((served, 8 * LANES), BF16),
-        pltpu.VMEM(turn.shape, F32),
-        pltpu.VMEM(mix.shape[1:], BF16),
-        pltpu.VMEM((8 * LANES, LANES), BF16),
-        pltpu.VMEM((served, cells), BF16),
-        pltpu.VMEM((group, vis), jnp.int32),
-        pltpu.SMEM((group, vis), jnp.int32),
-        sem((3 + served // 256,)),
-    ]
-    (own_sum,) = call(
-        functools.partial(share_body, partner=False),
-        [((served, cells), F32, FAST)],
-        [(me, pltpu.SMEM), (asked, FAST), (half, FAST), (turn, ANY), (mix, ANY)],
-        scratch,
-    )
     (partial,) = call(
-        functools.partial(share_body, partner=True),
+        share_body,
         [((served, cells), BF16, ANY)],
-        [(me, pltpu.SMEM), (asked, FAST), (other, FAST), (turn, ANY), (mix, ANY), (own_sum, FAST)],
-        scratch,
+        [
+            (me, pltpu.SMEM),
+            (asked, FAST),
+            (half, FAST),
+            (other, FAST),
+            (turn_fast, FAST),
+            (mix_fast, FAST),
+        ],
+        [
+            pltpu.VMEM((served, 16 * LANES), BF16),
+            pltpu.VMEM((16 * LANES, LANES), BF16),
+            pltpu.VMEM((served, cells), BF16),
+            pltpu.VMEM((group, vis), jnp.int32),
+            pltpu.SMEM((group, vis), jnp.int32),
+            sem((1 + served // 256,)),
+        ],
     )
     tiles = exchange(partial.reshape(group // 2, 2 * vis, cells), "bl")
     target, kernels_fast = call(

time: 105 us -> 102 us (0.971)
  blocking collectives: 13 us -> 22.6 us
  starting transfers between devices: 57.1 us -> 48.4 us
  Pallas kernels: 16.8 us -> 13.8 us
    all_to_all x1 -> x2, blocking collectives: 13 us -> 22.6 us  [exchange(): return lax.all_to_all(block, axes, split_axis=0, concat_axis=0, tiled=True)]
    all_to_all x2 -> x1, waiting for transfers between devices: 15.9 us -> 9.15 us  [exchange(): return lax.all_to_all(block, axes, split_axis=0, concat_axis=0, tiled=True)]
    ppermute x2, waiting for transfers between devices: 0.14 us -> 6.78 us  [the longest x1 6.12 us: on_device(): high = lax.ppermute(first, 'beam', backward)]
    ppermute x1, starting transfers between devices: 41.3 us -> 36.9 us  [on_device(): other = lax.ppermute(half, 'pol', [(0, 1), (1, 0)])]
    all_to_all x2 -> x1, starting transfers between devices: 7.26 us -> 3.63 us  [exchange(): return lax.all_to_all(block, axes, split_axis=0, concat_axis=0, tiled=True)]
    pallas_call x8 -> x6, Pallas kernels: 16.8 us -> 13.8 us  [call(): pl.pallas_call(body, out_shape=shapes, in_specs=[spec(space) for _, space...]
  transfers between devices with their start and end apart: 5 -> 4, of which waited for: 3 -> 3; matrix products, arithmetic and copies ran while one was open for 0% -> 0% of each run, Pallas kernels for 7% -> 2%
where the time goes in v5:
time: 102 us; the launch traced here: 101 us
  starting transfers between devices  48.4 us (47%)
  blocking collectives  22.6 us (22%)
  waiting for transfers between devices  15.9 us (16%)
  Pallas kernels  13.8 us (14%)
    ppermute x1, starting transfers between devices, on_device(): other = lax.ppermute(half, 'pol', [(0, 1), (1, 0)])  36.9 us
    all_to_all x2, blocking collectives, exchange(): return lax.all_to_all(block, axes, split_axis=0, concat_axis=0, tiled=True)  22.6 us
    pallas_call x6, Pallas kernels, call(): pl.pallas_call(body, out_shape=shapes, in_specs=[spec(space) for _, space...  13.8 us
    all_to_all x1, waiting for transfers between devices, exchange(): return lax.all_to_all(block, axes, split_axis=0, concat_axis=0, tiled=True)  9.15 us
    ppermute x1, starting transfers between devices, on_device(): low = lax.ppermute(last, 'beam', forward)  6.57 us
    ppermute x1, waiting for transfers between devices, on_device(): high = lax.ppermute(first, 'beam', backward)  6.12 us
    all_to_all x1, starting transfers between devices, exchange(): return lax.all_to_all(block, axes, split_axis=0, concat_axis=0, tiled=True)  3.63 us
  transfers between devices with their start and end apart: 4, of which 3 were waited for; matrix products, arithmetic and copies ran while one was open for 0% of the time, Pallas kernels for 2%

profile of v5, /device:TPU:65, one launch (start us, length us, event | category | flops | bytes accessed | tf_op | source)
XLA Modules:
  0.0 101.5 jit_solution(18115899937341591569)
XLA Ops:
  0.6 2.6 %shard_map.113 = (s32[16,64]{1,0:T(8,128)}, bf16[128,512]{1,0:T(8,128)(2,1)S(1)}, bf16[128,512]{1,0:T(8,128)(2,1)S(1)}, bf16[256,128]{1,0:T(8,128)(2,1)S(1)}, f3...) custom-call(s32[1]{0:T(128)} %bitcast.me_ref, ...), custom_call_target="tpu_custom_call" | custom-call | tf_op jit(solution)/shard_map/pallas_call | solution.py:347
  3.3 0.0 copy-start.1
  3.3 6.6 %collective-permute-start = (bf16[128,512]{1,0:T(8,128)(2,1)S(1)}, bf16[128,512]{1,0:T(8,128)(2,1)S(1)}, u32[]{:S(2)}, u32[]{:S(2)}) collective-permute-start(bf16[128,512]{1,0:T(8,128)(2,1)S(1)} %get-tuple-element.16), channel_id=1, source_target_pairs={{0,16},{16,32},{32,48},{48,64},{64,80},{80,96},{96,112},{112,128},... | collective-permute-start | bytes 393224 | tf_op jit(solution)/shard_map/ppermute | solution.py:399
  9.9 1.3 %collective-permute-start.1 = (bf16[128,512]{1,0:T(8,128)(2,1)S(1)}, bf16[128,512]{1,0:T(8,128)(2,1)S(1)}, u32[]{:S(2)}, u32[]{:S(2)}) collective-permute-start(bf16[128,512]{1,0:T(8,128)(2,1)S(1)} %get-tuple-element.18), channel_id=1, source_target_pairs={{16,0},{32,16},{48,32},{64,48},{80,64},{96,80},{112,96},{128,112},... | collective-permute-start | bytes 393224 | tf_op jit(solution)/shard_map/ppermute | solution.py:400
  11.2 0.7 collective-permute-done.low_ref
  11.8 6.1 %collective-permute-done.1.high_ref = bf16[128,512]{1,0:T(8,128)(2,1)S(1)} collective-permute-done((bf16[128,512]{1,0:T(8,128)(2,1)S(1)}, bf16[128,512]{1,0:T(8,128)(2,1)S(1)}, u32[]{:S(2)}, u32[]{:S(2)}) %collective-permute-start.1) | collective-permute-done | bytes 131104 | tf_op jit(solution)/shard_map/ppermute | solution.py:400
  18.0 2.2 %shard_map.114.own_ref = bf16[2048,128]{1,0:T(8,128)(2,1)S(1)} custom-call(bf16[128,512]{1,0:T(8,128)(2,1)S(1)} %collective-permute-done.low_ref, bf16[128,1024]{1,0:T(8,128)(2,1)S(1)} %get-tuple-element.17.sky_ref, bf16[128,512]{1,0:T(8,128)(2,1)S(1)} %collective-permute-done.1.high_ref, bf16[128,2048]{1,0:T(8,128)(2,1)S(1)} %get-tuple-element.19.pattern_ref, ...), custom_call_target="tpu_custom_call" | custom-call | tf_op jit(solution)/shard_map/pallas_call | solution.py:347
  20.2 36.9 %collective-permute-start.2 = (bf16[2048,128]{1,0:T(8,128)(2,1)S(1)}, bf16[2048,128]{1,0:T(8,128)(2,1)S(1)}, u32[]{:S(2)}, u32[]{:S(2)}) collective-permute-start(bf16[2048,128]{1,0:T(8,128)(2,1)S(1)} %shard_map.114.own_ref), channel_id=1, source_target_pairs={{0,1},{1,0},{2,3},{3,2},{4,5},{5,4},{6,7},{7,6},{8,9},{9,8},{10,11... | collective-permute-start | bytes 1572872 | tf_op jit(solution)/shard_map/ppermute | solution.py:415
  57.1 0.0 copy-done.1
  57.1 9.6 %all_to_all.21 = s32[16,1,64]{2,1,0:T(1,128)S(1)} all-to-all(s32[16,1,64]{2,1,0:T(1,128)S(1)} %bitcast.23), channel_id=1, replica_groups=mesh['tile'=2,'beam'=16,'bl'=8,'pol'=2] {'bl','pol'}, dimensions={0} | all-to-all | bytes 8192 | tf_op jit(solution)/shard_map/all_to_all | solution.py:357
  66.7 0.0 collective-permute-done.2.other_ref
  66.7 0.0 copy-start
  66.7 4.0 %shard_map.115 = bf16[1024,128]{1,0:T(8,128)(2,1)} custom-call(s32[1]{0:T(128)} %bitcast.me_ref, s32[16,64]{1,0:T(8,128)S(1)} %bitcast.15, bf16[2048,128]{1,0:T(8,128)(2,1)S(1)} %shard_map.114.own_ref, bf16[2048,128]{1,0:T(8,128)(2,1)S(1)} %collective-permute-done.2.other_ref, f32[2,128,128]{2,1,0:T(8,128)S(1)} %get-tuple-element.20.turn_ref, ...), custom_call_target="tpu_custom_call" | custom-call | tf_op jit(solution)/shard_map/pallas_call | solution.py:347
  70.7 3.6 %all-to-all-start.1 = ((bf16[8,128,128]{2,1,0:T(8,128)(2,1)}), bf16[8,128,128]{2,1,0:T(8,128)(2,1)S(1)}, u32[]{:S(2)}, u32[]{:S(2)}) async-start(bf16[8,128,128]{2,1,0:T(8,128)(2,1)} %bitcast.20), calls=%async_computation.1 | async-start | bytes 524288 | tf_op jit(solution)/shard_map/all_to_all | solution.py:357
  74.3 1.6 %shard_map.116 = (s32[1,256]{1,0:T(1,128)S(1)}, bf16[8192,128]{1,0:T(8,128)(2,1)S(1)}) custom-call(s32[1]{0:T(128)} %bitcast.me_ref, s32[16,64]{1,0:T(8,128)S(1)} %bitcast.16, bf16[8192,128]{1,0:T(8,128)(2,1)} %bitcast.18), custom_call_target="tpu_custom_call" | custom-call | tf_op jit(solution)/shard_map/pallas_call | solution.py:347
  76.0 9.2 %all-to-all-done.1.tiles_ref = bf16[8,128,128]{2,1,0:T(8,128)(2,1)S(1)} async-done(((bf16[8,128,128]{2,1,0:T(8,128)(2,1)}), bf16[8,128,128]{2,1,0:T(8,128)(2,1)S(1)}, u32[]{:S(2)}, u32[]{:S(2)}) %all-to-all-start.1) | async-done | bytes 262176 | tf_op jit(solution)/shard_map/all_to_all | solution.py:357
  85.1 0.0 copy-done
  85.1 2.1 %shard_map.117 = (f32[128,128]{1,0:T(8,128)}, bf16[256,128]{1,0:T(8,128)(2,1)}) custom-call(bf16[8,128,128]{2,1,0:T(8,128)(2,1)S(1)} %all-to-all-done.1.tiles_ref, bf16[256,128]{1,0:T(8,128)(2,1)S(1)} %get-tuple-element.22.put_ref, f32[128,128]{1,0:T(8,128)S(1)} %get-tuple-element.23.live_ref, f32[128,128]{1,0:T(8,128)S(1)} %bitcast.17, ...), custom_call_target="tpu_custom_call" | custom-call | tf_op jit(solution)/shard_map/pallas_call | solution.py:347
  87.2 13.0 %all_to_all.22 = bf16[16,16,128]{2,1,0:T(8,128)(2,1)S(1)} all-to-all(bf16[16,16,128]{2,1,0:T(8,128)(2,1)} %bitcast.22), channel_id=1, replica_groups=mesh['tile'=2,'beam'=16,'bl'=8,'pol'=2] {'bl','pol'}, dimensions={0} | all-to-all | bytes 131072 | tf_op jit(solution)/shard_map/all_to_all | solution.py:357
  100.3 1.2 %shard_map.118 = f32[2048,128]{1,0:T(8,128)} custom-call(bf16[256,128]{1,0:T(8,128)(2,1)S(1)} %bitcast.14, s32[1,256]{1,0:T(1,128)S(1)} %get-tuple-element.27.target_ref), custom_call_target="tpu_custom_call" | custom-call | tf_op jit(solution)/shard_map/pallas_call | solution.py:347
Async XLA Ops:
  3.3 53.8 %copy-start.1 = (s32[16,64]{1,0:T(8,128)S(1)}, s32[16,64]{1,0:T(8,128)}, u32[]{:S(2)}) copy-start(s32[16,64]{1,0:T(8,128)} %get-tuple-element.15) | copy-start | bytes 12292
  3.3 8.6 %collective-permute-start = (bf16[128,512]{1,0:T(8,128)(2,1)S(1)}, bf16[128,512]{1,0:T(8,128)(2,1)S(1)}, u32[]{:S(2)}, u32[]{:S(2)}) collective-permute-start(bf16[128,512]{1,0:T(8,128)(2,1)S(1)} %get-tuple-element.16), channel_id=1, source_target_pairs={{0,16},{16,32},{32,48},{48,64},{64,80},{80,96},{96,112},{112,128},... | collective-permute-start | bytes 393224 | tf_op jit(solution)/shard_map/ppermute | solution.py:399
  9.9 8.1 %collective-permute-start.1 = (bf16[128,512]{1,0:T(8,128)(2,1)S(1)}, bf16[128,512]{1,0:T(8,128)(2,1)S(1)}, u32[]{:S(2)}, u32[]{:S(2)}) collective-permute-start(bf16[128,512]{1,0:T(8,128)(2,1)S(1)} %get-tuple-element.18), channel_id=1, source_target_pairs={{16,0},{32,16},{48,32},{64,48},{80,64},{96,80},{112,96},{128,112},... | collective-permute-start | bytes 393224 | tf_op jit(solution)/shard_map/ppermute | solution.py:400
  20.2 46.5 %collective-permute-start.2 = (bf16[2048,128]{1,0:T(8,128)(2,1)S(1)}, bf16[2048,128]{1,0:T(8,128)(2,1)S(1)}, u32[]{:S(2)}, u32[]{:S(2)}) collective-permute-start(bf16[2048,128]{1,0:T(8,128)(2,1)S(1)} %shard_map.114.own_ref), channel_id=1, source_target_pairs={{0,1},{1,0},{2,3},{3,2},{4,5},{5,4},{6,7},{7,6},{8,9},{9,8},{10,11... | collective-permute-start | bytes 1572872 | tf_op jit(solution)/shard_map/ppermute | solution.py:415
  66.7 18.4 %copy-start = (f32[1,64,2,128]{3,2,1,0:T(2,128)S(1)}, f32[1,64,2,128]{3,2,1,0:T(2,128)}, u32[]{:S(2)}) copy-start(f32[1,64,2,128]{3,2,1,0:T(2,128)} %param.13) | copy-start | bytes 196612
  70.7 14.4 %all-to-all-start.1 = ((bf16[8,128,128]{2,1,0:T(8,128)(2,1)}), bf16[8,128,128]{2,1,0:T(8,128)(2,1)S(1)}, u32[]{:S(2)}, u32[]{:S(2)}) async-start(bf16[8,128,128]{2,1,0:T(8,128)(2,1)} %bitcast.20), calls=%async_computation.1 | async-start | bytes 524288 | tf_op jit(solution)/shard_map/all_to_all | solution.py:357
